TPU v7x, 512 devices: a whole 4x8x8 slice. The times are simulated.
512 devices in a mesh: tm: 64 (over z, y), space: 8 (over x, core).
Axes of the slice: x: 4, y: 8, z: 8, core: 2. Of those that a mesh axis runs over, the one named last changes fastest.
Arguments:
- links: float32 [2, 3, 3, 256, 32768], P(None, None, None, 'tm', 'space'), may hold values from -1 to 1, as said below
Outputs:
- ploop: float32 [2, 32768], P(None, ('space', 'tm'))
- loop_stats: float32 [3], replicated
Inputs may be any that keep to these rules, and one draw needn't show every extreme that they name: `links`: every link matrix is special unitary.
All inputs are finite; a program needn't handle non-finite values.
Results may differ from a plain program's by a relative error of at most 0.00014.
Values sent between devices are 32-bit elements; how exact they have to be, the bound alone decides.
A program may use at most 64 MiB of HBM per device.

v0:
```python
import jax
import jax.numpy as jnp
from jax import lax
from jax.sharding import Mesh
from jax.sharding import PartitionSpec as P

TM = ("tm_0", "tm_1")
SPACE_TM = ("space", "tm_0", "tm_1")


def cut_along(array, dim, count):
    dims = array.shape
    parts = array.reshape(*dims[:dim], count, dims[dim] // count, *dims[dim + 1 :])
    return jnp.moveaxis(parts, dim, 0)


def in_order(parts, dim):
    dims = list(parts.shape[1:])
    dims[dim] *= parts.shape[0]
    return jnp.moveaxis(parts, 0, dim).reshape(dims)


def exchange_in_order(parts, axes, order):
    dims = [lax.axis_size(a) for a in axes]
    parts = parts.reshape(*dims, *parts.shape[1:])
    for k in order:
        parts = lax.all_to_all(parts, axes[k], split_axis=k, concat_axis=k, tiled=True)
    return parts.reshape(-1, *parts.shape[len(axes) :])


def exchange_by_axis(array, axes, order, split_dim, concat_dim):
    parts = cut_along(array, split_dim, lax.axis_size(axes))
    return in_order(exchange_in_order(parts, axes, order), concat_dim)


def from_everyone(array, axis):
    count = lax.axis_size(axis)
    return lax.all_to_all(
        jnp.broadcast_to(array[None], (count, *array.shape)), axis, 0, 0, tiled=True
    )


def gathered_copies(array, axis, dim):
    return in_order(from_everyone(array, axis), dim)


def taken_together(array, axis):
    return from_everyone(array, axis).sum(axis=0)


def in_one(arrays, axis):
    flat, at, gathered = (jnp.concatenate([a.reshape(-1) for a in arrays]), 0, [])
    total = taken_together(flat, axis)
    for a in arrays:
        gathered.append(total[at : at + a.size].reshape(a.shape))
        at += a.size
    return tuple(gathered)


def cmul(left, right):

    def prod(first, second):
        return jnp.sum(first[:, :, None, :] * second[None, :, :, :], axis=1)

    return jnp.stack(
        [
            prod(left[0], right[0]) - prod(left[1], right[1]),
            prod(left[0], right[1]) + prod(left[1], right[0]),
        ]
    )


def trace_third(whole):
    return (whole[:, 0, 0] + whole[:, 1, 1] + whole[:, 2, 2]) / 3.0


def on_device(links):

    def step(index, acc):
        return cmul(acc, lax.dynamic_index_in_dim(links, index, 3, keepdims=False))

    local = lax.fori_loop(1, links.shape[3], step, links[:, :, :, 0, :])
    sites = links.shape[4]
    slabs = lax.axis_size(TM)
    grouped = exchange_by_axis(local[:, :, :, None, :], TM, (0, 1), 4, 3)

    def across(index, acc):
        return cmul(acc, lax.dynamic_index_in_dim(grouped, index, 3, keepdims=False))

    owned = trace_third(lax.fori_loop(1, slabs, across, grouped[:, :, :, 0, :]))
    ploop = gathered_copies(owned, TM, 1)
    total_sites = sites * lax.axis_size("space")
    sum_re, sum_im, sum_sq = in_one(
        (jnp.sum(ploop[0]), jnp.sum(ploop[1]), jnp.sum(ploop[0] * ploop[0] + ploop[1] * ploop[1])),
        "space",
    )
    mean_re = sum_re / total_sites
    mean_im = sum_im / total_sites
    square = sum_sq / total_sites
    stats = jnp.stack([mean_re, mean_im, square - mean_re * mean_re - mean_im * mean_im])
    return (owned, stats)


def solution(mesh):
    finer = Mesh(mesh.devices.reshape(8, 8, mesh.shape["space"]), ("tm_0", "tm_1", "space"))
    in_specs = (P(None, None, None, TM, "space"),)
    out_specs = (P(None, SPACE_TM), P())
    return jax.shard_map(
        on_device, mesh=finer, in_specs=in_specs, out_specs=out_specs, check_vma=False
    )
```

profile of v0, /device:TPU:1, one launch (start us, length us, event | category | flops | bytes accessed | tf_op | source)
XLA Modules:
  0.0 101.9 jit_solution(14077066839441528238)
XLA Ops:
  0.6 1.5 %slice.128 = f32[2,3,3,1,4096]{4,3,2,1,0:T(1,128)S(1)} slice(f32[2,3,3,4,4096]{4,3,2,1,0:T(4,128)} %param.5), slice={[0:2], [0:3], [0:3], [0:1], [0:4096]} | slice | bytes 589824 | tf_op jit(solution)/shard_map/slice | solution.py:82
  2.1 0.2 copy.90
  2.3 8.2 %while.30 = (s32[]{:T(128)}, f32[2,3,3,4096]{3,2,1,0:T(4,128)S(1)}, f32[2,3,3,4,4096]{4,3,2,1,0:T(4,128)}, s32[]{:T(128)}, s32[]{:T(128)}, /*index=5*/s32[]{:T(128)}, s32[]{}) while((s32[]{:T(128)}, f32[2,3,3,4096]{3,2,1,0:T(4,128)S(1)}, f32[2,3,3,4,4096]{4,3,2,1,0:T(4,128)}, s32[]{:T(128)}, s32[]{:T(128)}, /*index=5*/s32[]{:T(128)}, ...), condition=%wide.region_5.6_spmd, body=%wide.region_0.5_spmd.sunk | while | flops 884742 | bytes 4423819 | solution.py:82
  2.3 1.6 %constant_dynamic-slice_fusion.6 = (f32[1,3,3,1,4096]{4,3,2,1,0:T(1,128)S(1)}, f32[1,3,3,1,4096]{4,3,2,1,0:T(1,128)S(1)}) fusion(f32[2,3,3,4,4096]{4,3,2,1,0:T(4,128)} %get-tuple-element.345, s32[]{:T(128)S(6)} %select_n.24, s32[]{:T(128)S(6)} %add.152), kind=kLoop, calls=%fused_computation.11.clone.1 | loop fusion | bytes 589832 | tf_op jit(solution)/shard_map/while/body/eval_jaxpr/slice | solution.py:67
  3.9 0.2 copy_bitcast_fusion.12
  4.2 0.6 multiply_reduce_fusion.10
  5.1 1.6 %constant_dynamic-slice_fusion.6 = (f32[1,3,3,1,4096]{4,3,2,1,0:T(1,128)S(1)}, f32[1,3,3,1,4096]{4,3,2,1,0:T(1,128)S(1)}) fusion(f32[2,3,3,4,4096]{4,3,2,1,0:T(4,128)} %get-tuple-element.345, s32[]{:T(128)S(6)} %select_n.24, s32[]{:T(128)S(6)} %add.152), kind=kLoop, calls=%fused_computation.11.clone.1 | loop fusion | bytes 589832 | tf_op jit(solution)/shard_map/while/body/eval_jaxpr/slice | solution.py:67
  6.7 0.2 copy_bitcast_fusion.12
  6.9 0.6 multiply_reduce_fusion.10
  7.8 1.6 %constant_dynamic-slice_fusion.6 = (f32[1,3,3,1,4096]{4,3,2,1,0:T(1,128)S(1)}, f32[1,3,3,1,4096]{4,3,2,1,0:T(1,128)S(1)}) fusion(f32[2,3,3,4,4096]{4,3,2,1,0:T(4,128)} %get-tuple-element.345, s32[]{:T(128)S(6)} %select_n.24, s32[]{:T(128)S(6)} %add.152), kind=kLoop, calls=%fused_computation.11.clone.1 | loop fusion | bytes 589832 | tf_op jit(solution)/shard_map/while/body/eval_jaxpr/slice | solution.py:67
  9.4 0.2 copy_bitcast_fusion.12
  9.7 0.6 multiply_reduce_fusion.10
  10.6 0.2 copy.59
  10.8 0.4 reshape_broadcast_in_dim.3
  11.2 0.4 reshape.178
  11.6 21.6 %all_to_all.21 = f32[8,1,9216]{2,1,0:T(1,128)S(1)} all-to-all(f32[8,1,9216]{2,1,0:T(1,128)S(1)} %reshape.178), channel_id=1, replica_groups=mesh['tm_0'=8,'tm_1'=8,'space'=8] {'tm_0'}, dimensions={0} | all-to-all | bytes 589824 | tf_op jit(solution)/shard_map/all_to_all | solution.py:27
  33.2 0.5 broadcast.10
  33.7 1.2 %reduce.4 = f32[8,9216]{1,0:T(8,128)S(1)} reduce(f32[8,1,9216]{2,1,0:T(1,128)S(1)} %all_to_all.21, f32[]{:T(128)} %broadcast.10), dimensions={1}, to_apply=%all_to_all.13.reduce_sub_computation | reduce | bytes 589828 | tf_op jit(solution)/shard_map/all_to_all | solution.py:27
  35.1 0.2 copy.93
  35.3 1.1 %reshape.180 = f32[8,1,9216]{2,1,0:T(1,128)} reshape(f32[8,1,3,3,2,8,64]{6,5,4,3,2,1,0:T(8,128)S(1)} %bitcast.76) | data formatting | bytes 589824
  36.4 6.8 %all-to-all-start.1 = ((f32[8,1,9216]{2,1,0:T(1,128)}), f32[8,1,9216]{2,1,0:T(1,128)S(1)}, u32[]{:S(2)}, u32[]{:S(2)}) async-start(f32[8,1,9216]{2,1,0:T(1,128)} %reshape.180), calls=%async_computation.1 | async-start | bytes 589824 | tf_op jit(solution)/shard_map/all_to_all | solution.py:27
  43.2 9.8 %all-to-all-done.1 = f32[8,1,9216]{2,1,0:T(1,128)S(1)} async-done(((f32[8,1,9216]{2,1,0:T(1,128)}), f32[8,1,9216]{2,1,0:T(1,128)S(1)}, u32[]{:S(2)}, u32[]{:S(2)}) %all-to-all-start.1) | async-done | bytes 294944 | tf_op jit(solution)/shard_map/all_to_all | solution.py:27
  53.0 1.2 %reduce.5 = f32[8,9216]{1,0:T(8,128)S(1)} reduce(f32[8,1,9216]{2,1,0:T(1,128)S(1)} %all-to-all-done.1, f32[]{:T(128)} %broadcast.10), dimensions={1}, to_apply=%all_to_all.14.reduce_sub_computation | reduce | bytes 589828 | tf_op jit(solution)/shard_map/all_to_all | solution.py:27
  54.3 0.2 copy.89
  54.6 9.3 %while.31 = (s32[]{:T(128)}, f32[2,3,3,64]{3,2,1,0:T(4,128)S(1)}, f32[2,3,3,64,64]{4,3,2,1,0:T(8,128)S(1)}, s32[]{:T(128)}, s32[]{:T(128)}, /*index=5*/s32[]{:T(128)}, s32[]{}) while((s32[]{:T(128)}, f32[2,3,3,64]{3,2,1,0:T(4,128)S(1)}, f32[2,3,3,64,64]{4,3,2,1,0:T(8,128)S(1)}, s32[]{:T(128)}, s32[]{:T(128)}, /*index=5*/s32[]{:T(128)}, ...), condition=%wide.region_11.12_spmd, body=%wide.region_6.11_spmd.sunk | while | flops 13830 | bytes 69259 | solution.py:90
  64.1 17.2 %all_to_all.22 = f32[64,1,128]{2,1,0:T(1,128)S(1)} all-to-all(f32[64,1,128]{2,1,0:T(1,128)S(1)} %reshape.182), channel_id=1, replica_groups=mesh['tm_0'=8,'tm_1'=8,'space'=8] {'tm_0','tm_1'}, dimensions={0} | all-to-all | bytes 65536 | tf_op jit(solution)/shard_map/all_to_all | solution.py:38
  81.3 0.6 reduce.6
  82.0 0.7 slice_reduce_fusion.1
  82.7 2.0 %pad_maximum_fusion.2 = f32[3]{0:T(128)S(1)} fusion(f32[1]{0:T(128)} %bitcast.25, f32[1]{0:T(128)} %bitcast.24, f32[1]{0:T(128)} %bitcast.23), kind=kLoop, calls=%fused_computation.34 | loop fusion | flops 6 | bytes 24 | tf_op jit(solution)/shard_map/concatenate | solution.py:52
  84.7 11.5 %all_to_all.23 = f32[8,1,3]{2,1,0:T(1,128)S(1)} all-to-all(f32[8,1,3]{2,1,0:T(1,128)S(1)} %broadcast_in_dim.5), channel_id=1, replica_groups=mesh['tm_0'=8,'tm_1'=8,'space'=8] {'space'}, dimensions={0} | all-to-all | bytes 192 | tf_op jit(solution)/shard_map/all_to_all | solution.py:38
  96.2 0.6 fusion
  101.3 0.6 pad_maximum_fusion.3
  (468 shorter events, 6.3 us)
Async XLA Ops:
  36.4 16.6 %all-to-all-start.1 = ((f32[8,1,9216]{2,1,0:T(1,128)}), f32[8,1,9216]{2,1,0:T(1,128)S(1)}, u32[]{:S(2)}, u32[]{:S(2)}) async-start(f32[8,1,9216]{2,1,0:T(1,128)} %reshape.180), calls=%async_computation.1 | async-start | bytes 589824 | tf_op jit(solution)/shard_map/all_to_all | solution.py:27
  63.9 38.0 %copy-start = (f32[2,1,1,64]{3,2,1,0:T(1,128)}, f32[2,1,1,64]{3,2,1,0:T(1,128)S(1)}, u32[]{:S(2)}) copy-start(f32[2,1,1,64]{3,2,1,0:T(1,128)S(1)} %add_multiply_fusion) | copy-start | bytes 1540
where the time goes:
time: 102 us
  blocking collectives  50.3 us (49%)
  local copies, waits for them, and re-layouts  13.1 us (13%)
  other arithmetic  12 us (12%)
  waiting for transfers between devices  9.76 us (10%)
  starting transfers between devices  6.82 us (7%)
  between operations  5.38 us (5%)
  loops' own time  4.63 us (5%)
    all_to_all x2, blocking collectives, from_everyone(): lax.all_to_all(jnp.broadcast_to(array[None], (count, *array.shape)), axis...  28.7 us
    all_to_all x1, blocking collectives, exchange_in_order(): lax.all_to_all(parts, axes[k], split_axis=k, concat_axis=k, tiled=True)  21.6 us
    all_to_all x1, waiting for transfers between devices, exchange_in_order(): lax.all_to_all(parts, axes[k], split_axis=k, concat_axis=k, tiled=True)  9.76 us
    all_to_all x1, starting transfers between devices, exchange_in_order(): lax.all_to_all(parts, axes[k], split_axis=k, concat_axis=k, tiled=True)  6.82 us
    slice x66, local copies, waits for them, and re-layouts, cmul(): right[0]  5.89 us
    another operation x1, loops' own time, on_device(): owned = trace_third(lax.fori_loop(1, slabs, across, grouped[:, :, :, 0, :]))  4.41 us
    reduce_sum x66, other arithmetic, prod(): return jnp.sum(first[:, :, None, :] * second[None, :, :, :], axis=1)  3.89 us
    all_to_all x2, other arithmetic, exchange_in_order(): lax.all_to_all(parts, axes[k], split_axis=k, concat_axis=k, tiled=True)  2.47 us
  transfers between devices with their start and end apart: 1, of which 1 were waited for; matrix products, arithmetic and copies ran while one was open for 0% of the time, Pallas kernels for 0%

commit v1 on v0

v1 whole, which is shorter than its diff:
```python
import jax
import jax.numpy as jnp
from jax import lax
from jax.experimental import pallas as pl
from jax.experimental.pallas import tpu as pltpu
from jax.sharding import PartitionSpec as P

MESH = pl.DeviceIdType.MESH
LANES = 128
NY = 8
NZ = 8
NCLASS = 4
NSPACE = 8
ROWS = 2
FAR_FIRST = (4, 3, 5, 2, 6, 1, 7)
PAIRS = (2, 1, 3, 0)


def third_row(a, b):
    row = []
    for i, j in ((1, 2), (2, 0), (0, 1)):
        re = (a[i][0] * b[j][0] - a[i][1] * b[j][1]) - (a[j][0] * b[i][0] - a[j][1] * b[i][1])
        im = (a[j][0] * b[i][1] + a[j][1] * b[i][0]) - (a[i][0] * b[j][1] + a[i][1] * b[j][0])
        row.append((re, im))
    return row


def times(left, right):
    out = []
    for row in left:
        new = []
        for c in range(3):
            re = im = None
            for k in range(3):
                lr, li = row[k]
                rr, ri = right[k][c]
                tr = lr * rr - li * ri
                ti = lr * ri + li * rr
                re = tr if re is None else re + tr
                im = ti if im is None else im + ti
            new.append((re, im))
        out.append(new)
    return out


def full(two):
    return [two[0], two[1], third_row(two[0], two[1])]


def kernel(links, ploop_out, stats_out, lbuf, ysend, yrecv, zsend, zrecv, prow, arecv, brecv,
           load_sem, ysend_sem, yrecv_sem, zsend_sem, zrecv_sem, psend_sem, precv_sem,
           asend_sem, arecv_sem, bsend_sem, brecv_sem):
    tm = lax.axis_index("tm")
    s = lax.axis_index("space")
    z = lax.div(tm, NY)
    y = lax.rem(tm, NY)

    def at(dz, dy, ds):
        return (lax.rem(z + dz + NZ, NZ) * NY + lax.rem(y + dy, NY), lax.rem(s + ds, NSPACE))

    loads = {}
    for k in range(4):
        for t in range(4):
            m = lax.rem(lax.div(y, 2) + PAIRS[k], 4)
            loads[k, t] = pltpu.make_async_copy(
                links.at[:, :, m, t], lbuf.at[k, t], load_sem.at[k, t])
            loads[k, t].start()

    barrier = pltpu.get_barrier_semaphore()

    def greet(where):
        pl.semaphore_signal(barrier, inc=1, device_id=where, device_id_type=MESH)

    for d in FAR_FIRST:
        greet(at(0, d, 0))
    for d in FAR_FIRST:
        greet(at(d, 0, 0))
    for dz in (0, 1, -1, 2):
        for d in range(1, NSPACE):
            greet(at(dz, 0, d))

    def local(k):
        for t in range(4):
            loads[k, t].wait()

        def matrix(t, rows):
            return [[(lbuf[k, t, r * 3 + c], lbuf[k, t, 9 + r * 3 + c]) for c in range(3)]
                    for r in range(rows)]

        acc = matrix(0, ROWS)
        for t in range(1, 4):
            acc = times(acc, matrix(t, 3))
        for h in range(2):
            for r in range(ROWS):
                for c in range(3):
                    for p in range(2):
                        ysend[k, h, (r * 3 + c) * 2 + p] = acc[r][c][p][4 * h:4 * h + 4]

    def ycopy(k, h, owner):
        return pltpu.make_async_remote_copy(
            src_ref=ysend.at[k, h], dst_ref=yrecv.at[y],
            send_sem=ysend_sem.at[k, h], recv_sem=yrecv_sem.at[y],
            device_id=(z * NY + owner, s), device_id_type=MESH)

    for k in range(4):
        local(k)
        if k == 0:
            pl.semaphore_wait(barrier, 2 * 7 + 4 * (NSPACE - 1))
        m = lax.rem(lax.div(y, 2) + PAIRS[k], 4)
        for h in range(2):
            owner = m * 2 + h
            if k < 3:
                ycopy(k, h, owner).start()
            else:
                @pl.when(owner != y)
                def _():
                    ycopy(k, h, owner).start()

                @pl.when(owner == y)
                def _():
                    yrecv[y] = ysend[k, h]

    acc = None
    for j in range(NY):
        @pl.when(y != j)
        def _():
            pltpu.make_async_remote_copy(
                src_ref=ysend.at[0, 0], dst_ref=yrecv.at[j],
                send_sem=ysend_sem.at[0, 0], recv_sem=yrecv_sem.at[j],
                device_id=(tm, s), device_id_type=MESH).wait_recv()

        two = [[(yrecv[j, (r * 3 + c) * 2], yrecv[j, (r * 3 + c) * 2 + 1]) for c in range(3)]
               for r in range(ROWS)]
        acc = two if acc is None else times(acc, full(two))
    for r in range(ROWS):
        for c in range(3):
            for p in range(2):
                zsend[(r * 3 + c) * 2 + p] = acc[r][c][p].reshape(4, 1, LANES)

    cls = lax.rem(z, NCLASS)
    zrecv[:, pl.ds(z, 1)] = zsend[:, pl.ds(cls, 1)]

    def zcopy(d):
        want = lax.rem(z + d, NCLASS)
        return pltpu.make_async_remote_copy(
            src_ref=zsend.at[:, want], dst_ref=zrecv.at[:, z],
            send_sem=zsend_sem.at[d], recv_sem=zrecv_sem,
            device_id=at(d, 0, 0), device_id_type=MESH)

    for d in FAR_FIRST:
        zcopy(d).start()
    rest = zrecv.at[:, pl.ds(0, NZ - 1)]
    pltpu.make_async_copy(rest, rest, zrecv_sem).wait()

    acc = None
    for j in range(NZ):
        two = [[(zrecv[(r * 3 + c) * 2, j], zrecv[(r * 3 + c) * 2 + 1, j]) for c in range(3)]
               for r in range(ROWS)]
        acc = two if acc is None else times(acc, full(two))
    whole = full(acc)
    re = (whole[0][0][0] + whole[1][1][0] + whole[2][2][0]) / 3.0
    im = (whole[0][0][1] + whole[1][1][1] + whole[2][2][1]) / 3.0

    half = lax.rem(y, 2)
    holder = lax.div(z, NCLASS) == half
    pcopy = pltpu.make_async_remote_copy(
        src_ref=prow, dst_ref=prow, send_sem=psend_sem, recv_sem=precv_sem,
        device_id=(tm + 1 - 2 * half, s), device_id_type=MESH)

    @pl.when(holder)
    def _():
        prow[0:1] = re
        prow[1:2] = im
        pcopy.start()

    lane = lax.broadcasted_iota(jnp.int32, (1, LANES), 1)
    sums = jnp.where(lane == 0, jnp.sum(re, axis=1, keepdims=True),
                     jnp.where(lane == 1, jnp.sum(im, axis=1, keepdims=True),
                               jnp.sum(re * re + im * im, axis=1, keepdims=True)))
    arecv[y] = sums

    def acopy(d):
        return pltpu.make_async_remote_copy(
            src_ref=arecv.at[y], dst_ref=arecv.at[y], send_sem=asend_sem.at[d],
            recv_sem=arecv_sem, device_id=at(0, d, 0), device_id_type=MESH)

    for d in FAR_FIRST:
        acopy(d).start()
    rest_a = arecv.at[pl.ds(0, NY - 1)]
    pltpu.make_async_copy(rest_a, rest_a, arecv_sem).wait()
    total = jnp.sum(arecv[...], axis=0)
    mine = cls * NSPACE + s
    brecv[mine] = total

    def bcopy(i, dz, d):
        return pltpu.make_async_remote_copy(
            src_ref=brecv.at[mine], dst_ref=brecv.at[mine], send_sem=bsend_sem.at[i],
            recv_sem=brecv_sem, device_id=at(dz, 0, d), device_id_type=MESH)

    bcopies = [bcopy(i * NSPACE + d, dz, d)
               for i, dz in enumerate((-2, -1, 1, 0)) for d in range(NSPACE) if dz != 0 or d != 0]
    for copy in bcopies:
        copy.start()

    @pl.when(jnp.logical_not(holder))
    def _():
        pcopy.wait_recv()

    both = prow[...]
    ploop_out[...] = jnp.where(half == 0, both[:, :64], both[:, 64:])

    rest_b = brecv.at[pl.ds(0, NCLASS * NSPACE - 1)]
    pltpu.make_async_copy(rest_b, rest_b, brecv_sem).wait()
    grand = jnp.sum(brecv[...], axis=0) / (NY * NCLASS * NSPACE * LANES)
    mean_re = grand[0, 0]
    mean_im = grand[0, 1]
    square = grand[0, 2]
    stats_out[0] = mean_re
    stats_out[1] = mean_im
    stats_out[2] = square - mean_re * mean_re - mean_im * mean_im

    for k in range(4):
        m = lax.rem(lax.div(y, 2) + PAIRS[k], 4)
        for h in range(2):
            if k < 3:
                ycopy(k, h, m * 2 + h).wait_send()
            else:
                @pl.when(m * 2 + h != y)
                def _():
                    ycopy(k, h, m * 2 + h).wait_send()
    for d in FAR_FIRST:
        zcopy(d).wait_send()
        acopy(d).wait_send()
    for copy in bcopies:
        copy.wait_send()

    @pl.when(holder)
    def _():
        pcopy.wait_send()


def on_device(links):
    times_here, sites = links.shape[3:]
    rows = sites // LANES
    view = links.reshape(18, times_here, rows, LANES).transpose(0, 2, 1, 3)
    view = view.reshape(18, 8, 4, times_here, LANES)
    f32 = jnp.float32
    dma = pltpu.SemaphoreType.DMA
    return pl.pallas_call(
        kernel,
        out_shape=(jax.ShapeDtypeStruct((2, sites // 64), f32), jax.ShapeDtypeStruct((3,), f32)),
        in_specs=[pl.BlockSpec(memory_space=pl.ANY)],
        out_specs=(pl.BlockSpec(memory_space=pltpu.VMEM), pl.BlockSpec(memory_space=pltpu.SMEM)),
        scratch_shapes=[
            pltpu.VMEM((4, 4, 18, 8, LANES), f32),
            pltpu.VMEM((4, 2, 12, 4, LANES), f32),
            pltpu.VMEM((NY, 12, 4, LANES), f32),
            pltpu.VMEM((12, 4, 1, LANES), f32),
            pltpu.VMEM((12, NZ, 1, LANES), f32),
            pltpu.VMEM((2, LANES), f32),
            pltpu.VMEM((NY, 1, LANES), f32),
            pltpu.VMEM((NCLASS * NSPACE, 1, LANES), f32),
            dma((4, 4)), dma((4, 2)), dma((NY,)), dma((NZ,)), dma, dma, dma,
            dma((NY,)), dma, dma((NCLASS * NSPACE,)), dma,
        ],
        compiler_params=pltpu.CompilerParams(collective_id=0, has_side_effects=True),
    )(view)


def solution(mesh):
    return jax.shard_map(
        on_device, mesh=mesh, in_specs=(P(None, None, None, "tm", "space"),),
        out_specs=(P(None, ("space", "tm")), P()), check_vma=False)
```

time: 102 us -> 40 us (0.39)
  blocking collectives: 50.3 us -> 0 us
  Pallas kernels: 0 us -> 36.8 us
  other arithmetic: 12 us -> 0 us
  local copies, waits for them, and re-layouts: 13.1 us -> 2.36 us
  waiting for transfers between devices: 9.76 us -> 0 us
  starting transfers between devices: 6.82 us -> 0 us
  between operations: 5.38 us -> 0.64 us
  loops' own time: 4.63 us -> 0 us
    all_to_all x3 -> x0, blocking collectives: 50.3 us -> none  [the longest x2 28.7 us: from_everyone(): lax.all_to_all(jnp.broadcast_to(array[None], (count, *array.shape)), axis...]
    pallas_call x0 -> x1, Pallas kernels: none -> 36.8 us  [on_device(): pl.pallas_call(kernel, out_shape=(jax.ShapeDtypeStruct((2, sites // 64),...]
    all_to_all x1 -> x0, waiting for transfers between devices: 9.76 us -> none  [exchange_in_order(): lax.all_to_all(parts, axes[k], split_axis=k, concat_axis=k, tiled=True)]
    slice x70 -> x0, local copies, waits for them, and re-layouts: 7.99 us -> none  [the longest x66 5.89 us: cmul(): right[0]]
    all_to_all x1 -> x0, starting transfers between devices: 6.82 us -> none  [exchange_in_order(): lax.all_to_all(parts, axes[k], split_axis=k, concat_axis=k, tiled=True)]
    another operation x2 -> x0, loops' own time: 4.63 us -> none  [the longest x1 4.41 us: on_device(): owned = trace_third(lax.fori_loop(1, slabs, across, grouped[:, :, :, 0, :]))]
    reduce_sum x68 -> x0, other arithmetic: 4.61 us -> none  [the longest x66 3.89 us: prod(): return jnp.sum(first[:, :, None, :] * second[None, :, :, :], axis=1)]
    all_to_all x3 -> x0, other arithmetic: 3.09 us -> none  [the longest x2 2.47 us: exchange_in_order(): lax.all_to_all(parts, axes[k], split_axis=k, concat_axis=k, tiled=True)]
  transfers between devices with their start and end apart: 1 -> 0, of which waited for: 1 -> 0; matrix products, arithmetic and copies ran while one was open for 0% -> 0% of each run, Pallas kernels for 0% -> 0%
where the time goes in v1:
time: 40 us; the launch traced here: 39.8 us
  Pallas kernels  36.8 us (92%)
  local copies, waits for them, and re-layouts  2.36 us (6%)
  between operations  0.64 us (2%)
    pallas_call x1, Pallas kernels, on_device(): pl.pallas_call(kernel, out_shape=(jax.ShapeDtypeStruct((2, sites // 64),...  36.8 us
    unnamed x2, local copies, waits for them, and re-layouts  2.36 us

profile of v1, /device:TPU:1, one launch (start us, length us, event | category | flops | bytes accessed | tf_op | source)
XLA Modules:
  0.0 39.8 jit_solution(11529244173773270271)
XLA Ops:
  0.6 36.8 %shard_map.30 = (f32[2,64]{1,0:T(2,128)}, f32[3]{0:T(128)}) custom-call(f32[18,8,4,4,128]{4,3,2,1,0:T(4,128)} %bitcast.5), custom_call_target="tpu_custom_call" | custom-call | tf_op jit(solution)/shard_map/pallas_call | solution.py:249
  37.5 1.2 %copy.6 = f32[2,64]{1,0:T(2,128)} copy(f32[2,64]{1,0:T(2,128)} %get-tuple-element.4) | data formatting | bytes 1024
  38.7 1.1 %copy.7 = f32[3]{0:T(128)} copy(f32[3]{0:T(128)} %get-tuple-element.5) | data formatting | bytes 24

commit v2 on v1

v2 whole, which is shorter than its diff:
```python
import jax
import jax.numpy as jnp
from jax import lax
from jax.experimental import pallas as pl
from jax.experimental.pallas import tpu as pltpu
from jax.sharding import PartitionSpec as P

MESH = pl.DeviceIdType.MESH
LANES = 128
NY = 8
NZ = 8
NCLASS = 4
NSPACE = 8
ROWS = 2
FAR_FIRST = (4, 3, 5, 2, 6, 1, 7)
PAIRS = (2, 1, 3, 0)


def third_row(a, b):
    row = []
    for i, j in ((1, 2), (2, 0), (0, 1)):
        re = (a[i][0] * b[j][0] - a[i][1] * b[j][1]) - (a[j][0] * b[i][0] - a[j][1] * b[i][1])
        im = (a[j][0] * b[i][1] + a[j][1] * b[i][0]) - (a[i][0] * b[j][1] + a[i][1] * b[j][0])
        row.append((re, im))
    return row


def times(left, right):
    out = []
    for row in left:
        new = []
        for c in range(3):
            re = im = None
            for k in range(3):
                lr, li = row[k]
                rr, ri = right[k][c]
                tr = lr * rr - li * ri
                ti = lr * ri + li * rr
                re = tr if re is None else re + tr
                im = ti if im is None else im + ti
            new.append((re, im))
        out.append(new)
    return out


def full(two):
    return [two[0], two[1], third_row(two[0], two[1])]


def kernel(links, ploop_out, stats_out, lbuf, ysend, yrecv, zsend, zrecv, prow, arecv, brecv,
           near_sem, load_sem, ysend_sem, yrecv_sem, zsend_sem, zrecv_sem, psend_sem, precv_sem,
           asend_sem, arecv_sem, bsend_sem, brecv_sem):
    tm = lax.axis_index("tm")
    s = lax.axis_index("space")
    z = lax.div(tm, NY)
    y = lax.rem(tm, NY)

    def at(dz, dy, ds):
        return (lax.rem(z + dz + NZ, NZ) * NY + lax.rem(y + dy + NY, NY), lax.rem(s + ds + NSPACE, NSPACE))

    other_core = (tm, s + 1 - 2 * lax.rem(s, 2))
    near = [at(1, 0, 0), at(-1, 0, 0), at(0, 0, 2), at(0, 0, -2), other_core]
    farther = [at(2, 0, 0), at(-2, 0, 0), at(0, 0, 4), other_core]

    def tell(sem, whom):
        for where in whom:
            pl.semaphore_signal(sem, inc=1, device_id=where, device_id_type=MESH)

    barrier = pltpu.get_barrier_semaphore()
    greeted = [at(0, d, 0) for d in FAR_FIRST] + near
    tell(barrier, greeted)

    pairs = [lax.rem(lax.div(y, 2) + step, 4) for step in PAIRS]
    for k, m in enumerate(pairs):
        for t in range(4):
            pltpu.make_async_copy(links.at[:, :, m, t], lbuf.at[k, t], load_sem.at[k]).start()

    def local(k):
        pltpu.make_async_copy(lbuf.at[k], lbuf.at[k], load_sem.at[k]).wait()

        def matrix(t, rows):
            return [[(lbuf[k, t, r * 3 + c], lbuf[k, t, 9 + r * 3 + c]) for c in range(3)]
                    for r in range(rows)]

        acc = matrix(0, ROWS)
        for t in range(1, 4):
            acc = times(acc, matrix(t, 3))
        for h in range(2):
            for r in range(ROWS):
                for c in range(3):
                    for p in range(2):
                        ysend[pairs[k] * 2 + h, (r * 3 + c) * 2 + p] = acc[r][c][p][4 * h:4 * h + 4]

    def ycopy(d):
        owner = lax.rem(y + d + NY, NY)
        pltpu.make_async_remote_copy(
            src_ref=ysend.at[owner], dst_ref=yrecv.at[y], send_sem=ysend_sem,
            recv_sem=yrecv_sem.at[y], device_id=(z * NY + owner, s), device_id_type=MESH).start()

    for k in range(4):
        local(k)
    pl.semaphore_wait(barrier, len(greeted))
    tell(near_sem.at[0], near)
    for d in FAR_FIRST:
        ycopy(d)
    yrecv[y] = ysend[y]
    pl.semaphore_wait(near_sem.at[0], len(near))
    tell(near_sem.at[1], farther)

    acc = None
    for j in range(NY):
        @pl.when(y != j)
        def _():
            pltpu.make_async_remote_copy(
                src_ref=ysend.at[0], dst_ref=yrecv.at[j],
                send_sem=ysend_sem, recv_sem=yrecv_sem.at[j],
                device_id=(tm, s), device_id_type=MESH).wait_recv()

        two = [[(yrecv[j, (r * 3 + c) * 2], yrecv[j, (r * 3 + c) * 2 + 1]) for c in range(3)]
               for r in range(ROWS)]
        acc = two if acc is None else times(acc, full(two))
    for r in range(ROWS):
        for c in range(3):
            for p in range(2):
                zsend[(r * 3 + c) * 2 + p] = acc[r][c][p].reshape(4, 1, LANES)

    pl.semaphore_wait(near_sem.at[1], len(farther))
    tell(near_sem.at[2], [other_core])
    cls = lax.rem(z, NCLASS)
    zrecv[:, pl.ds(z, 1)] = zsend[:, pl.ds(cls, 1)]

    def zcopy(d):
        want = lax.rem(z + d, NCLASS)
        return pltpu.make_async_remote_copy(
            src_ref=zsend.at[:, want], dst_ref=zrecv.at[:, z],
            send_sem=zsend_sem, recv_sem=zrecv_sem,
            device_id=at(d, 0, 0), device_id_type=MESH)

    for d in FAR_FIRST:
        zcopy(d).start()
    rest = zrecv.at[:, pl.ds(0, NZ - 1)]
    pltpu.make_async_copy(rest, rest, zrecv_sem).wait()
    acc = None
    for j in range(NZ):
        two = [[(zrecv[(r * 3 + c) * 2, j], zrecv[(r * 3 + c) * 2 + 1, j]) for c in range(3)]
               for r in range(ROWS)]
        acc = two if acc is None else times(acc, full(two))
    whole = full(acc)
    re = (whole[0][0][0] + whole[1][1][0] + whole[2][2][0]) / 3.0
    im = (whole[0][0][1] + whole[1][1][1] + whole[2][2][1]) / 3.0

    half = lax.rem(y, 2)
    holder = lax.div(z, NCLASS) == half
    pcopy = pltpu.make_async_remote_copy(
        src_ref=prow, dst_ref=prow, send_sem=psend_sem, recv_sem=precv_sem,
        device_id=(tm + 1 - 2 * half, s), device_id_type=MESH)

    @pl.when(holder)
    def _():
        prow[0:1] = re
        prow[1:2] = im
        pcopy.start()

    lane = lax.broadcasted_iota(jnp.int32, (1, LANES), 1)
    sums = jnp.where(lane == 0, jnp.sum(re, axis=1, keepdims=True),
                     jnp.where(lane == 1, jnp.sum(im, axis=1, keepdims=True),
                               jnp.sum(re * re + im * im, axis=1, keepdims=True)))
    arecv[y] = sums

    def acopy(d):
        return pltpu.make_async_remote_copy(
            src_ref=arecv.at[y], dst_ref=arecv.at[y], send_sem=asend_sem,
            recv_sem=arecv_sem, device_id=at(0, d, 0), device_id_type=MESH)

    for d in FAR_FIRST:
        acopy(d).start()
    rest_a = arecv.at[pl.ds(0, NY - 1)]
    pltpu.make_async_copy(rest_a, rest_a, arecv_sem).wait()
    total = jnp.sum(arecv[...], axis=0)
    mine = cls * NSPACE + s
    brecv[mine] = total

    def bcopy(dz, d):
        return pltpu.make_async_remote_copy(
            src_ref=brecv.at[mine], dst_ref=brecv.at[mine], send_sem=bsend_sem,
            recv_sem=brecv_sem, device_id=at(dz, 0, d), device_id_type=MESH)

    pl.semaphore_wait(near_sem.at[2], 1)
    for dz in (2, -1, 1, 0):
        for d in range(NSPACE):
            if dz != 0 or d != 0:
                bcopy(dz, d).start()

    @pl.when(jnp.logical_not(holder))
    def _():
        pcopy.wait_recv()

    ploop_out[...] = jnp.where(half == 0, prow[:, :64], prow[:, 64:])

    rest_b = brecv.at[pl.ds(0, NCLASS * NSPACE - 1)]
    pltpu.make_async_copy(rest_b, rest_b, brecv_sem).wait()
    grand = jnp.sum(brecv[...], axis=0) / (NY * NCLASS * NSPACE * LANES)
    means = jnp.where(lane < 2, grand * grand, 0.0)
    stats = grand - jnp.where(lane == 2, jnp.sum(means, axis=1, keepdims=True), 0.0)
    stats_out[...] = stats[0, :3]

    for ref, sem in ((ysend.at[pl.ds(0, NY - 1)], ysend_sem), (rest, zsend_sem), (rest_a, asend_sem), (rest_b, bsend_sem)):
        pltpu.make_async_remote_copy(
            src_ref=ref, dst_ref=ref, send_sem=sem, recv_sem=sem,
            device_id=other_core, device_id_type=MESH).wait_send()

    @pl.when(holder)
    def _():
        pcopy.wait_send()


def finish(ploop_in, stats_in, ploop_out, stats_out, sems):
    copies = [pltpu.make_async_copy(ploop_in, ploop_out, sems.at[0]),
              pltpu.make_async_copy(stats_in, stats_out, sems.at[1])]
    for copy in copies:
        copy.start()
    for copy in copies:
        copy.wait()


def on_device(links):
    times_here, sites = links.shape[3:]
    rows = sites // LANES
    view = links.reshape(18, times_here, rows, LANES).transpose(0, 2, 1, 3)
    view = view.reshape(18, 8, 4, times_here, LANES)
    f32 = jnp.float32
    dma = pltpu.SemaphoreType.DMA
    vmem = pl.BlockSpec(memory_space=pltpu.VMEM)
    ploop, stats = pl.pallas_call(
        kernel,
        out_shape=(pltpu.VMEM((2, sites // 64), f32), pltpu.VMEM((3,), f32)),
        in_specs=[pl.BlockSpec(memory_space=pl.ANY)],
        out_specs=(vmem, vmem),
        scratch_shapes=[
            pltpu.VMEM((4, 4, 18, 8, LANES), f32),
            pltpu.VMEM((NY, 12, 4, LANES), f32),
            pltpu.VMEM((NY, 12, 4, LANES), f32),
            pltpu.VMEM((12, 4, 1, LANES), f32),
            pltpu.VMEM((12, NZ, 1, LANES), f32),
            pltpu.VMEM((2, LANES), f32),
            pltpu.VMEM((NY, 1, LANES), f32),
            pltpu.VMEM((NCLASS * NSPACE, 1, LANES), f32),
            pltpu.SemaphoreType.REGULAR((3,)),
            dma((4,)), dma, dma((NY,)), dma, dma, dma, dma, dma, dma, dma, dma,
        ],
        compiler_params=pltpu.CompilerParams(collective_id=0, has_side_effects=True),
    )(view)
    hbm = pl.BlockSpec(memory_space=pl.ANY)
    return pl.pallas_call(
        finish,
        out_shape=(jax.ShapeDtypeStruct((2, sites // 64), f32), jax.ShapeDtypeStruct((3,), f32)),
        in_specs=[vmem, vmem],
        out_specs=(hbm, hbm),
        scratch_shapes=[dma((2,))],
    )(*(pltpu.with_memory_space_constraint(x, pltpu.VMEM) for x in (ploop, stats)))


def solution(mesh):
    return jax.shard_map(
        on_device, mesh=mesh, in_specs=(P(None, None, None, "tm", "space"),),
        out_specs=(P(None, ("space", "tm")), P()), check_vma=False)
```

time: 40 us -> 36.1 us (0.903)
  local copies, waits for them, and re-layouts: 2.36 us -> 0 us
  Pallas kernels: 36.8 us -> 35.3 us
    unnamed x2 -> x0, local copies, waits for them, and re-layouts: 2.36 us -> none
    pallas_call x1 -> x2, Pallas kernels: 36.8 us -> 35.3 us  [the longest x1 34.7 us: on_device(): pl.pallas_call(kernel, out_shape=(pltpu.VMEM((2, sites // 64), f32), pltp...]
where the time goes in v2:
time: 36.1 us; the launch traced here: 35.9 us
  Pallas kernels  35.3 us (98%)
  between operations  0.64 us (2%)
    pallas_call x1, Pallas kernels, on_device(): pl.pallas_call(kernel, out_shape=(pltpu.VMEM((2, sites // 64), f32), pltp...  34.7 us

profile of v2, /device:TPU:1, one launch (start us, length us, event | category | flops | bytes accessed | tf_op | source)
XLA Modules:
  0.0 35.9 jit_solution(10098133045968029470)
XLA Ops:
  0.6 34.7 %shard_map.30 = (f32[2,64]{1,0:T(2,128)S(1)}, f32[3]{0:T(128)S(1)}) custom-call(f32[18,8,4,4,128]{4,3,2,1,0:T(4,128)} %bitcast.5), custom_call_target="tpu_custom_call" | custom-call | tf_op jit(solution)/shard_map/pallas_call | solution.py:234
  35.3 0.6 %shard_map.31 = (f32[2,64]{1,0:T(2,128)}, f32[3]{0:T(128)}) custom-call(f32[2,64]{1,0:T(2,128)S(1)} %get-tuple-element.4.ploop_in, f32[3]{0:T(128)S(1)} %get-tuple-element.5.stats_in), custom_call_target="tpu_custom_call" | custom-call | tf_op jit(solution)/shard_map/pallas_call | solution.py:254

commit v3 on v2

v3 whole, which is shorter than its diff:
```python
import jax
import jax.numpy as jnp
from jax import lax
from jax.experimental import pallas as pl
from jax.experimental.pallas import tpu as pltpu
from jax.sharding import PartitionSpec as P

MESH = pl.DeviceIdType.MESH
LANES = 128
NY = 8
NZ = 8
NCLASS = 4
NX = 4
NSPACE = 8
ROWS = 2
FAR_FIRST = (4, 3, 5, 2, 6, 1, 7)
PAIRS = (2, 1, 3, 0)


def third_row(a, b):
    row = []
    for i, j in ((1, 2), (2, 0), (0, 1)):
        re = (a[i][0] * b[j][0] - a[i][1] * b[j][1]) - (a[j][0] * b[i][0] - a[j][1] * b[i][1])
        im = (a[j][0] * b[i][1] + a[j][1] * b[i][0]) - (a[i][0] * b[j][1] + a[i][1] * b[j][0])
        row.append((re, im))
    return row


def times(left, right):
    out = []
    for row in left:
        new = []
        for c in range(3):
            re = im = None
            for k in range(3):
                lr, li = row[k]
                rr, ri = right[k][c]
                tr = lr * rr - li * ri
                ti = lr * ri + li * rr
                re = tr if re is None else re + tr
                im = ti if im is None else im + ti
            new.append((re, im))
        out.append(new)
    return out


def full(two):
    return [two[0], two[1], third_row(two[0], two[1])]


def kernel(links, ploop_out, stats_out, lbuf, ysend, yrecv, zsend, zrecv, phold, prow, arecv, brecv,
           near_sem, load_sem, ysend_sem, yrecv_sem, zsend_sem, zrecv_sem, psend_sem, precv_sem,
           asend_sem, arecv_sem, bsend_sem, brecv_sem):
    tm = lax.axis_index("tm")
    s = lax.axis_index("space")
    z = lax.div(tm, NY)
    y = lax.rem(tm, NY)
    x = lax.div(s, 2)
    core = lax.rem(s, 2)

    def at(dz, dy, dx, to):
        return (lax.rem(z + dz + NZ, NZ) * NY + lax.rem(y + dy + NY, NY), lax.rem(x + dx, NX) * 2 + to)

    def tell(sem, whom):
        for where in whom:
            pl.semaphore_signal(sem, inc=1, device_id=where, device_id_type=MESH)

    ring = [at(0, d, 0, 1) for d in FAR_FIRST]
    near = [at(1, 0, 0, 1), at(-1, 0, 0, 1), at(0, 0, 1, 1), at(0, 0, 3, 1)]
    farther = [at(2, 0, 0, 1), at(-2, 0, 0, 1), at(0, 0, 2, 1)]
    barrier = pltpu.get_barrier_semaphore()

    @pl.when(core == 1)
    def _():
        tell(barrier, ring + [at(0, d, 0, 0) for d in FAR_FIRST] + near + [at(0, 0, 0, 0)])

    @pl.when(core == 0)
    def _():
        tell(barrier, [at(0, 0, 0, 1)])

    pairs = [lax.rem(lax.div(y, 2) + step, 4) for step in PAIRS]
    for k, m in enumerate(pairs):
        for t in range(4):
            pltpu.make_async_copy(links.at[:, :, m, t], lbuf.at[k, t], load_sem.at[k]).start()

    def local(k):
        pltpu.make_async_copy(lbuf.at[k], lbuf.at[k], load_sem.at[k]).wait()

        def matrix(t, rows):
            return [[(lbuf[k, t, r * 3 + c], lbuf[k, t, 9 + r * 3 + c]) for c in range(3)]
                    for r in range(rows)]

        acc = matrix(0, ROWS)
        for t in range(1, 4):
            acc = times(acc, matrix(t, 3))
        for h in range(2):
            for r in range(ROWS):
                for c in range(3):
                    for p in range(2):
                        ysend[pairs[k] * 2 + h, (r * 3 + c) * 2 + p] = acc[r][c][p][4 * h:4 * h + 4]

    def ycopy(d):
        owner = lax.rem(y + d, NY)
        pltpu.make_async_remote_copy(
            src_ref=ysend.at[owner], dst_ref=yrecv.at[y, :, pl.ds(pl.multiple_of(core * NCLASS, NCLASS), NCLASS)],
            send_sem=ysend_sem, recv_sem=yrecv_sem.at[y, core], device_id=at(0, d, 0, 1), device_id_type=MESH).start()

    for k in range(4):
        local(k)

    def sent(ref, sem):
        pltpu.make_async_remote_copy(
            src_ref=ref, dst_ref=ref, send_sem=sem, recv_sem=sem,
            device_id=at(0, 0, 0, 1 - core), device_id_type=MESH).wait_send()

    def arrived(ref, sem):
        pltpu.make_async_copy(ref, ref, sem).wait()

    half = lax.rem(y, 2)
    holder = lax.div(z, NCLASS) == half
    lane = lax.broadcasted_iota(jnp.int32, (1, LANES), 1)

    @pl.when(core == 0)
    def _():
        pl.semaphore_wait(barrier, NY)
        for d in FAR_FIRST + (0,):
            ycopy(d)
        arrived(prow, precv_sem)
        arrived(brecv, brecv_sem)
        sent(ysend, ysend_sem)

    @pl.when(core == 1)
    def _():
        pl.semaphore_wait(barrier, len(ring) + len(near) + 1)
        tell(near_sem.at[0], near)
        for d in FAR_FIRST:
            ycopy(d)
        yrecv[y, :, NCLASS:] = ysend[y]
        pl.semaphore_wait(near_sem.at[0], len(near))
        tell(near_sem.at[1], farther)

        acc = None
        for j in range(NY):
            arrived(yrecv.at[j, :, pl.ds(0, NCLASS)], yrecv_sem.at[j, 0])

            @pl.when(y != j)
            def _():
                arrived(yrecv.at[j, :, pl.ds(NCLASS, NCLASS)], yrecv_sem.at[j, 1])

            two = [[(yrecv[j, (r * 3 + c) * 2], yrecv[j, (r * 3 + c) * 2 + 1]) for c in range(3)]
                   for r in range(ROWS)]
            acc = two if acc is None else times(acc, full(two))
        for r in range(ROWS):
            for c in range(3):
                for p in range(2):
                    for i in range(NCLASS):
                        for to in range(2):
                            row = NCLASS * to + i
                            zsend[(r * 3 + c) * 2 + p, i, to:to + 1] = acc[r][c][p][row:row + 1]

        pl.semaphore_wait(near_sem.at[1], len(farther))
        tell(near_sem.at[2], [at(0, 0, 2, 1)])
        cls = lax.rem(z, NCLASS)
        for d in FAR_FIRST:
            pltpu.make_async_remote_copy(
                src_ref=zsend.at[:, lax.rem(z + d, NCLASS)], dst_ref=zrecv.at[:, z],
                send_sem=zsend_sem, recv_sem=zrecv_sem, device_id=at(d, 0, 0, 1), device_id_type=MESH).start()
        zrecv[:, z] = zsend[:, cls]
        arrived(zrecv.at[:, pl.ds(0, NZ - 1)], zrecv_sem)

        acc = None
        for j in range(NZ):
            two = [[(zrecv[(r * 3 + c) * 2, j], zrecv[(r * 3 + c) * 2 + 1, j]) for c in range(3)]
                   for r in range(ROWS)]
            acc = two if acc is None else times(acc, full(two))
        whole = full(acc)
        re = (whole[0][0][0] + whole[1][1][0] + whole[2][2][0]) / 3.0
        im = (whole[0][0][1] + whole[1][1][1] + whole[2][2][1]) / 3.0

        def total(value):
            return jnp.sum(jnp.sum(value, axis=1, keepdims=True), axis=0, keepdims=True)

        sums = jnp.where(lane == 0, total(re), jnp.where(lane == 1, total(im), total(re * re + im * im)))
        arecv[y] = sums
        for d in FAR_FIRST:
            pltpu.make_async_remote_copy(
                src_ref=arecv.at[y], dst_ref=arecv.at[y], send_sem=asend_sem,
                recv_sem=arecv_sem, device_id=at(0, d, 0, 1), device_id_type=MESH).start()

        @pl.when(holder)
        def _():
            for to in range(2):
                phold[to, 0:1] = re[to:to + 1]
                phold[to, 1:2] = im[to:to + 1]
            other = 1 - 2 * half
            for to, where in ((0, (tm, s - 1)), (0, (tm + other, s - 1)), (1, (tm + other, s))):
                pltpu.make_async_remote_copy(
                    src_ref=phold.at[to], dst_ref=prow, send_sem=psend_sem, recv_sem=precv_sem,
                    device_id=where, device_id_type=MESH).start()
            prow[...] = phold[1]

        arrived(arecv.at[pl.ds(0, NY - 1)], arecv_sem)
        mine = cls * NX + x
        brecv[mine] = jnp.sum(arecv[...], axis=0)
        pl.semaphore_wait(near_sem.at[2], 1)
        for dz in (2, -1, 1, 0):
            for dx in (2, 1, 3, 0):
                for to in (0, 1):
                    if dz != 0 or dx != 0 or to == 0:
                        pltpu.make_async_remote_copy(
                            src_ref=brecv.at[mine], dst_ref=brecv.at[mine], send_sem=bsend_sem,
                            recv_sem=brecv_sem, device_id=at(dz, 0, dx, to), device_id_type=MESH).start()

        @pl.when(jnp.logical_not(holder))
        def _():
            arrived(prow, precv_sem)

        arrived(brecv.at[pl.ds(0, NCLASS * NX - 1)], brecv_sem)
        sent(ysend.at[pl.ds(0, NY - 1)], ysend_sem)
        sent(zrecv.at[:, pl.ds(0, NZ - 1)], zsend_sem)
        sent(arecv.at[pl.ds(0, NY - 1)], asend_sem)
        sent(brecv, bsend_sem)
        sent(brecv.at[pl.ds(0, NCLASS * NX - 1)], bsend_sem)

        @pl.when(holder)
        def _():
            for _ in range(3):
                sent(prow, psend_sem)

    ploop_out[...] = jnp.where(half == 0, prow[:, :64], prow[:, 64:])
    grand = jnp.sum(brecv[...], axis=0) / (NY * NCLASS * NSPACE * LANES)
    means = jnp.where(lane < 2, grand * grand, 0.0)
    stats = grand - jnp.where(lane == 2, jnp.sum(means, axis=1, keepdims=True), 0.0)
    stats_out[...] = stats[0, :3]


def finish(ploop_in, stats_in, ploop_out, stats_out, sems):
    copies = [pltpu.make_async_copy(ploop_in, ploop_out, sems.at[0]),
              pltpu.make_async_copy(stats_in, stats_out, sems.at[1])]
    for copy in copies:
        copy.start()
    for copy in copies:
        copy.wait()


def on_device(links):
    times_here, sites = links.shape[3:]
    rows = sites // LANES
    view = links.reshape(18, times_here, rows, LANES).transpose(0, 2, 1, 3)
    view = view.reshape(18, 8, 4, times_here, LANES)
    f32 = jnp.float32
    dma = pltpu.SemaphoreType.DMA
    vmem = pl.BlockSpec(memory_space=pltpu.VMEM)
    ploop, stats = pl.pallas_call(
        kernel,
        out_shape=(pltpu.VMEM((2, sites // 64), f32), pltpu.VMEM((3,), f32)),
        in_specs=[pl.BlockSpec(memory_space=pl.ANY)],
        out_specs=(vmem, vmem),
        scratch_shapes=[
            pltpu.VMEM((4, 4, 18, 8, LANES), f32),
            pltpu.VMEM((NY, 12, NCLASS, LANES), f32),
            pltpu.VMEM((NY, 12, 2 * NCLASS, LANES), f32),
            pltpu.VMEM((12, NCLASS, 2, LANES), f32),
            pltpu.VMEM((12, NZ, 2, LANES), f32),
            pltpu.VMEM((2, 2, LANES), f32),
            pltpu.VMEM((2, LANES), f32),
            pltpu.VMEM((NY, 1, LANES), f32),
            pltpu.VMEM((NCLASS * NX, 1, LANES), f32),
            pltpu.SemaphoreType.REGULAR((3,)),
            dma((4,)), dma, dma((NY, 2)), dma, dma, dma, dma, dma, dma, dma, dma,
        ],
        compiler_params=pltpu.CompilerParams(collective_id=0, has_side_effects=True),
    )(view)
    hbm = pl.BlockSpec(memory_space=pl.ANY)
    return pl.pallas_call(
        finish,
        out_shape=(jax.ShapeDtypeStruct((2, sites // 64), f32), jax.ShapeDtypeStruct((3,), f32)),
        in_specs=[vmem, vmem],
        out_specs=(hbm, hbm),
        scratch_shapes=[dma((2,))],
    )(*(pltpu.with_memory_space_constraint(x, pltpu.VMEM) for x in (ploop, stats)))


def solution(mesh):
    return jax.shard_map(
        on_device, mesh=mesh, in_specs=(P(None, None, None, "tm", "space"),),
        out_specs=(P(None, ("space", "tm")), P()), check_vma=False)
```

time: 36.1 us -> 33.8 us (0.936)
  Pallas kernels: 35.3 us -> 33 us
    pallas_call x1, Pallas kernels: 34.7 us -> 32.4 us  [on_device(): pl.pallas_call(kernel, out_shape=(pltpu.VMEM((2, sites // 64), f32), pltp...]
where the time goes in v3:
time: 33.8 us; the launch traced here: 33.6 us
  Pallas kernels  33 us (98%)
  between operations  0.64 us (2%)
    pallas_call x1, Pallas kernels, on_device(): pl.pallas_call(kernel, out_shape=(pltpu.VMEM((2, sites // 64), f32), pltp...  32.4 us

profile of v3, /device:TPU:1, one launch (start us, length us, event | category | flops | bytes accessed | tf_op | source)
XLA Modules:
  0.0 33.6 jit_solution(16157525037618200420)
XLA Ops:
  0.6 32.4 %shard_map.30 = (f32[2,64]{1,0:T(2,128)S(1)}, f32[3]{0:T(128)S(1)}) custom-call(f32[18,8,4,4,128]{4,3,2,1,0:T(4,128)} %bitcast.5), custom_call_target="tpu_custom_call" | custom-call | tf_op jit(solution)/shard_map/pallas_call | solution.py:254
  33.0 0.6 %shard_map.31 = (f32[2,64]{1,0:T(2,128)}, f32[3]{0:T(128)}) custom-call(f32[2,64]{1,0:T(2,128)S(1)} %get-tuple-element.4.ploop_in, f32[3]{0:T(128)S(1)} %get-tuple-element.5.stats_in), custom_call_target="tpu_custom_call" | custom-call | tf_op jit(solution)/shard_map/pallas_call | solution.py:275

commit v4 on v3

--- a/solution.py
+++ b/solution.py
@@ -13,6 +13,7 @@
 NX = 4
 NSPACE = 8
 ROWS = 2
+COORDS = 8
 FAR_FIRST = (4, 3, 5, 2, 6, 1, 7)
 PAIRS = (2, 1, 3, 0)
 
@@ -24,6 +25,66 @@
         im = (a[j][0] * b[i][1] + a[j][1] * b[i][0]) - (a[i][0] * b[j][1] + a[i][1] * b[j][0])
         row.append((re, im))
     return row
+
+
+def product(a, b):
+    return (a[0] * b[0] - a[1] * b[1], a[0] * b[1] + a[1] * b[0])
+
+
+def conj_product(a, b):
+    return (a[0] * b[0] + a[1] * b[1], a[0] * b[1] - a[1] * b[0])
+
+
+def project(p):
+    q = p[1] * p[1]
+    for v in p[2:]:
+        q = q + v * v
+    below = p[0] < 0.0
+    scale = jnp.where(below, 1.0 - p[0], 1.0) / jnp.where(below, jnp.maximum(q, 1e-20), 1.0 + p[0])
+    return [jnp.where(below & (q < 1e-20), 1e-10, p[1]) * scale] + [v * scale for v in p[2:]]
+
+
+def weight(x):
+    n = x[0] * x[0]
+    for v in x[1:]:
+        n = n + v * v
+    return 2.0 / (1.0 + n)
+
+
+def lift(x):
+    w = weight(x)
+    return [w - 1.0] + [w * v for v in x]
+
+
+def reflector(x):
+    r = weight(x) / (1.0 + x[0] * x[0])
+    return (r, r * x[0]), [(1.0, x[0]), (x[1], x[2]), (x[3], x[4])]
+
+
+def coordinates(two):
+    a, b = two
+    x = project([v for pair in a for v in pair])
+    h, u = reflector(x)
+    parts = [conj_product(u[k], b[k]) for k in range(3)]
+    k = conj_product(h, (parts[0][0] + parts[1][0] + parts[2][0], parts[0][1] + parts[1][1] + parts[2][1]))
+    rest = []
+    for j in (1, 2):
+        off = product(u[j], k)
+        rest += [b[j][0] - off[0], b[j][1] - off[1]]
+    return x + project(rest)
+
+
+def first_rows(v):
+    x = v[:5]
+    p = lift(x)
+    q = lift(v[5:])
+    h, u = reflector(x)
+    one = conj_product(u[1], (q[0], q[1]))
+    two = conj_product(u[2], (q[2], q[3]))
+    g = product(h, (one[0] + two[0], one[1] + two[1]))
+    off = [product(g, u[k]) for k in range(3)]
+    return [[(p[0], p[1]), (p[2], p[3]), (p[4], p[5])],
+            [(-off[0][0], -off[0][1]), (q[0] - off[1][0], q[1] - off[1][1]), (q[2] - off[2][0], q[3] - off[2][1])]]
 
 
 def times(left, right):
@@ -48,7 +109,7 @@
     return [two[0], two[1], third_row(two[0], two[1])]
 
 
-def kernel(links, ploop_out, stats_out, lbuf, ysend, yrecv, zsend, zrecv, phold, prow, arecv, brecv,
+def kernel(links, ploop_out, stats_out, lbuf, ysend, yrecv, ymat, zsend, zrecv, zmat, phold, prow, arecv, brecv,
            near_sem, load_sem, ysend_sem, yrecv_sem, zsend_sem, zrecv_sem, psend_sem, precv_sem,
            asend_sem, arecv_sem, bsend_sem, brecv_sem):
     tm = lax.axis_index("tm")
@@ -93,11 +154,9 @@
         acc = matrix(0, ROWS)
         for t in range(1, 4):
             acc = times(acc, matrix(t, 3))
-        for h in range(2):
-            for r in range(ROWS):
-                for c in range(3):
-                    for p in range(2):
-                        ysend[pairs[k] * 2 + h, (r * 3 + c) * 2 + p] = acc[r][c][p][4 * h:4 * h + 4]
+        for i, v in enumerate(coordinates(acc)):
+            for h in range(2):
+                ysend[pairs[k] * 2 + h, i] = v[4 * h:4 * h + 4]
 
     def ycopy(d):
         owner = lax.rem(y + d, NY)
@@ -107,6 +166,15 @@
 
     for k in range(4):
         local(k)
+
+    def store(ref, j, mat):
+        for r in range(3):
+            for c in range(3):
+                for p in range(2):
+                    ref[j, (r * 3 + c) * 2 + p] = mat[r][c][p]
+
+    def load(ref, j):
+        return [[(ref[j, (r * 3 + c) * 2], ref[j, (r * 3 + c) * 2 + 1]) for c in range(3)] for r in range(3)]
 
     def sent(ref, sem):
         pltpu.make_async_remote_copy(
@@ -139,40 +207,45 @@
         pl.semaphore_wait(near_sem.at[0], len(near))
         tell(near_sem.at[1], farther)
 
-        acc = None
-        for j in range(NY):
+        for d in FAR_FIRST + (0,):
+            j = lax.rem(y + d, NY)
             arrived(yrecv.at[j, :, pl.ds(0, NCLASS)], yrecv_sem.at[j, 0])
-
-            @pl.when(y != j)
-            def _():
+            if d != 0:
                 arrived(yrecv.at[j, :, pl.ds(NCLASS, NCLASS)], yrecv_sem.at[j, 1])
-
-            two = [[(yrecv[j, (r * 3 + c) * 2], yrecv[j, (r * 3 + c) * 2 + 1]) for c in range(3)]
-                   for r in range(ROWS)]
-            acc = two if acc is None else times(acc, full(two))
-        for r in range(ROWS):
-            for c in range(3):
-                for p in range(2):
-                    for i in range(NCLASS):
-                        for to in range(2):
-                            row = NCLASS * to + i
-                            zsend[(r * 3 + c) * 2 + p, i, to:to + 1] = acc[r][c][p][row:row + 1]
+            store(ymat, j, full(first_rows([yrecv[j, i] for i in range(COORDS)])))
+        acc = load(ymat, 0)[:ROWS]
+        for j in range(1, NY):
+            acc = times(acc, load(ymat, j))
+        for i, v in enumerate(coordinates(acc)):
+            for k in range(NCLASS):
+                for to in range(2):
+                    row = NCLASS * to + k
+                    zsend[i, k, to:to + 1] = v[row:row + 1]
 
         pl.semaphore_wait(near_sem.at[1], len(farther))
         tell(near_sem.at[2], [at(0, 0, 2, 1)])
         cls = lax.rem(z, NCLASS)
         for d in FAR_FIRST:
             pltpu.make_async_remote_copy(
-                src_ref=zsend.at[:, lax.rem(z + d, NCLASS)], dst_ref=zrecv.at[:, z],
+                src_ref=zsend.at[:, lax.rem(z + d, NCLASS)], dst_ref=zrecv.at[:, pl.ds(z * 2, 2)],
                 send_sem=zsend_sem, recv_sem=zrecv_sem, device_id=at(d, 0, 0, 1), device_id_type=MESH).start()
-        zrecv[:, z] = zsend[:, cls]
-        arrived(zrecv.at[:, pl.ds(0, NZ - 1)], zrecv_sem)
-
-        acc = None
-        for j in range(NZ):
-            two = [[(zrecv[(r * 3 + c) * 2, j], zrecv[(r * 3 + c) * 2 + 1, j]) for c in range(3)]
-                   for r in range(ROWS)]
-            acc = two if acc is None else times(acc, full(two))
+        zrecv[:, pl.ds(z * 2, 2)] = zsend[:, cls]
+        arrived(zrecv.at[:, pl.ds(0, 2 * NZ - 2)], zrecv_sem)
+
+        for j in range(2):
+            mat = full(first_rows([zrecv[i, 8 * j:8 * j + 8] for i in range(COORDS)]))
+            for r in range(3):
+                for c in range(3):
+                    for p in range(2):
+                        zmat[(r * 3 + c) * 2 + p, 8 * j:8 * j + 8] = mat[r][c][p]
+
+        def slab(j):
+            return [[tuple(zmat[(r * 3 + c) * 2 + p, 2 * j:2 * j + 2] for p in range(2)) for c in range(3)]
+                    for r in range(3)]
+
+        acc = slab(0)[:ROWS]
+        for j in range(1, NZ):
+            acc = times(acc, slab(j))
         whole = full(acc)
         re = (whole[0][0][0] + whole[1][1][0] + whole[2][2][0]) / 3.0
         im = (whole[0][0][1] + whole[1][1][1] + whole[2][2][1]) / 3.0
@@ -217,7 +290,7 @@
 
         arrived(brecv.at[pl.ds(0, NCLASS * NX - 1)], brecv_sem)
         sent(ysend.at[pl.ds(0, NY - 1)], ysend_sem)
-        sent(zrecv.at[:, pl.ds(0, NZ - 1)], zsend_sem)
+        sent(zrecv.at[:, pl.ds(0, 2 * NZ - 2)], zsend_sem)
         sent(arecv.at[pl.ds(0, NY - 1)], asend_sem)
         sent(brecv, bsend_sem)
         sent(brecv.at[pl.ds(0, NCLASS * NX - 1)], bsend_sem)
@@ -258,10 +331,12 @@
         out_specs=(vmem, vmem),
         scratch_shapes=[
             pltpu.VMEM((4, 4, 18, 8, LANES), f32),
-            pltpu.VMEM((NY, 12, NCLASS, LANES), f32),
-            pltpu.VMEM((NY, 12, 2 * NCLASS, LANES), f32),
-            pltpu.VMEM((12, NCLASS, 2, LANES), f32),
-            pltpu.VMEM((12, NZ, 2, LANES), f32),
+            pltpu.VMEM((NY, COORDS, NCLASS, LANES), f32),
+            pltpu.VMEM((NY, COORDS, 2 * NCLASS, LANES), f32),
+            pltpu.VMEM((NY, 18, 2 * NCLASS, LANES), f32),
+            pltpu.VMEM((COORDS, NCLASS, 2, LANES), f32),
+            pltpu.VMEM((COORDS, 2 * NZ, LANES), f32),
+            pltpu.VMEM((18, 2 * NZ, LANES), f32),
             pltpu.VMEM((2, 2, LANES), f32),
             pltpu.VMEM((2, LANES), f32),
             pltpu.VMEM((NY, 1, LANES), f32),

time: 33.8 us -> 33.2 us (0.982)
  Pallas kernels: 33 us -> 32.4 us
    pallas_call x1, Pallas kernels: 32.4 us -> 31.8 us  [on_device(): pl.pallas_call(kernel, out_shape=(pltpu.VMEM((2, sites // 64), f32), pltp...]
where the time goes in v4:
time: 33.2 us; the launch traced here: 33 us
  Pallas kernels  32.4 us (98%)
  between operations  0.64 us (2%)
    pallas_call x1, Pallas kernels, on_device(): pl.pallas_call(kernel, out_shape=(pltpu.VMEM((2, sites // 64), f32), pltp...  31.8 us

profile of v4, /device:TPU:1, one launch (start us, length us, event | category | flops | bytes accessed | tf_op | source)
XLA Modules:
  0.0 33.0 jit_solution(10251172851182953774)
XLA Ops:
  0.6 31.8 %shard_map.30 = (f32[2,64]{1,0:T(2,128)S(1)}, f32[3]{0:T(128)S(1)}) custom-call(f32[18,8,4,4,128]{4,3,2,1,0:T(4,128)} %bitcast.5), custom_call_target="tpu_custom_call" | custom-call | tf_op jit(solution)/shard_map/pallas_call | solution.py:327
  32.5 0.6 %shard_map.31 = (f32[2,64]{1,0:T(2,128)}, f32[3]{0:T(128)}) custom-call(f32[2,64]{1,0:T(2,128)S(1)} %get-tuple-element.4.ploop_in, f32[3]{0:T(128)S(1)} %get-tuple-element.5.stats_in), custom_call_target="tpu_custom_call" | custom-call | tf_op jit(solution)/shard_map/pallas_call | solution.py:350

commit v5 on v4

--- a/solution.py
+++ b/solution.py
@@ -15,6 +15,8 @@
 ROWS = 2
 COORDS = 8
 FAR_FIRST = (4, 3, 5, 2, 6, 1, 7)
+Z_ORDER = (0, 7, 6, 1, 5, 2, 4, 3)
+RELAYED = ((0, 4, 2, 0, (1,)), (0, 4, 6, 1, (0,)), (0, 5, 6, 0, (0, 1)), (7, 4, 5, 0, (0, 1)))
 PAIRS = (2, 1, 3, 0)
 
 
@@ -109,8 +111,8 @@
     return [two[0], two[1], third_row(two[0], two[1])]
 
 
-def kernel(links, ploop_out, stats_out, lbuf, ysend, yrecv, ymat, zsend, zrecv, zmat, phold, prow, arecv, brecv,
-           near_sem, load_sem, ysend_sem, yrecv_sem, zsend_sem, zrecv_sem, psend_sem, precv_sem,
+def kernel(links, ploop_out, stats_out, lbuf, ysend, yvia, yrecv, ymat, zsend, zrecv, zmat, phold, prow, arecv, brecv,
+           near_sem, load_sem, via_sem, vsend_sem, ysend_sem, yrecv_sem, zsend_sem, zrecv_sem, psend_sem, precv_sem,
            asend_sem, arecv_sem, bsend_sem, brecv_sem):
     tm = lax.axis_index("tm")
     s = lax.axis_index("space")
@@ -126,14 +128,25 @@
         for where in whom:
             pl.semaphore_signal(sem, inc=1, device_id=where, device_id_type=MESH)
 
-    ring = [at(0, d, 0, 1) for d in FAR_FIRST]
+    def relayed(start, end):
+        found = False
+        for i, j in {(r[0], r[1]): 0 for r in RELAYED}:
+            found = found | ((start == i) & (end == j))
+        return found
+
+    direct = NY - 1 - sum(jnp.where(y == i, 1, 0) for i, _ in {(r[0], r[1]): 0 for r in RELAYED})
     near = [at(1, 0, 0, 1), at(-1, 0, 0, 1), at(0, 0, 1, 1), at(0, 0, 3, 1)]
     farther = [at(2, 0, 0, 1), at(-2, 0, 0, 1), at(0, 0, 2, 1)]
     barrier = pltpu.get_barrier_semaphore()
 
     @pl.when(core == 1)
     def _():
-        tell(barrier, ring + [at(0, d, 0, 0) for d in FAR_FIRST] + near + [at(0, 0, 0, 0)])
+        for d in FAR_FIRST:
+            @pl.when(jnp.logical_not(relayed(lax.rem(y + d, NY), y)))
+            def _():
+                tell(barrier, [at(0, d, 0, 1), at(0, d, 0, 0)])
+
+        tell(barrier, near + [at(0, 0, 0, 0)])
 
     @pl.when(core == 0)
     def _():
@@ -158,14 +171,35 @@
             for h in range(2):
                 ysend[pairs[k] * 2 + h, i] = v[4 * h:4 * h + 4]
 
-    def ycopy(d):
-        owner = lax.rem(y + d, NY)
+    def ycopy(q):
         pltpu.make_async_remote_copy(
-            src_ref=ysend.at[owner], dst_ref=yrecv.at[y, :, pl.ds(pl.multiple_of(core * NCLASS, NCLASS), NCLASS)],
-            send_sem=ysend_sem, recv_sem=yrecv_sem.at[y, core], device_id=at(0, d, 0, 1), device_id_type=MESH).start()
+            src_ref=ysend.at[q], dst_ref=yrecv.at[y, :, pl.ds(pl.multiple_of(core * NCLASS, NCLASS), NCLASS)],
+            send_sem=ysend_sem, recv_sem=yrecv_sem.at[y, core], device_id=(z * NY + q, x * 2 + 1), device_id_type=MESH).start()
 
     for k in range(4):
         local(k)
+        if k == 0:
+            pl.semaphore_wait(barrier, jnp.where(core == 1, direct + len(near) + 1, direct + 1))
+
+            @pl.when(core == 1)
+            def _():
+                tell(near_sem.at[0], near)
+
+        for start, end, by, slot, cores in RELAYED:
+            if k == (2 if start == 7 else 0):
+                @pl.when((y == start) & ((core == cores[0]) | (core == cores[-1])))
+                def _():
+                    pltpu.make_async_remote_copy(
+                        src_ref=ysend.at[end], dst_ref=yvia.at[slot, core], send_sem=ysend_sem,
+                        recv_sem=via_sem.at[slot, core], device_id=(z * NY + by, x * 2 + 1),
+                        device_id_type=MESH).start()
+
+        for h in range(2):
+            q = pairs[k] * 2 + h
+
+            @pl.when(jnp.logical_not(relayed(y, q)) & ((q != y) | (core == 0)))
+            def _():
+                ycopy(q)
 
     def store(ref, j, mat):
         for r in range(3):
@@ -190,22 +224,25 @@
 
     @pl.when(core == 0)
     def _():
-        pl.semaphore_wait(barrier, NY)
-        for d in FAR_FIRST + (0,):
-            ycopy(d)
         arrived(prow, precv_sem)
         arrived(brecv, brecv_sem)
         sent(ysend, ysend_sem)
 
     @pl.when(core == 1)
     def _():
-        pl.semaphore_wait(barrier, len(ring) + len(near) + 1)
-        tell(near_sem.at[0], near)
-        for d in FAR_FIRST:
-            ycopy(d)
         yrecv[y, :, NCLASS:] = ysend[y]
         pl.semaphore_wait(near_sem.at[0], len(near))
         tell(near_sem.at[1], farther)
+
+        for start, end, by, slot, cores in RELAYED:
+            @pl.when(y == by)
+            def _():
+                for to in cores:
+                    arrived(yvia.at[slot, to], via_sem.at[slot, to])
+                    pltpu.make_async_remote_copy(
+                        src_ref=yvia.at[slot, to], dst_ref=yrecv.at[start, :, pl.ds(NCLASS * to, NCLASS)],
+                        send_sem=vsend_sem, recv_sem=yrecv_sem.at[start, to], device_id=(z * NY + end, s),
+                        device_id_type=MESH).start()
 
         for d in FAR_FIRST + (0,):
             j = lax.rem(y + d, NY)
@@ -220,19 +257,23 @@
             for k in range(NCLASS):
                 for to in range(2):
                     row = NCLASS * to + k
-                    zsend[i, k, to:to + 1] = v[row:row + 1]
+                    at_row = k // 2 * 2 + to
+                    zsend[i, k % 2, at_row:at_row + 1] = v[row:row + 1]
 
         pl.semaphore_wait(near_sem.at[1], len(farther))
         tell(near_sem.at[2], [at(0, 0, 2, 1)])
-        cls = lax.rem(z, NCLASS)
-        for d in FAR_FIRST:
-            pltpu.make_async_remote_copy(
-                src_ref=zsend.at[:, lax.rem(z + d, NCLASS)], dst_ref=zrecv.at[:, pl.ds(z * 2, 2)],
-                send_sem=zsend_sem, recv_sem=zrecv_sem, device_id=at(d, 0, 0, 1), device_id_type=MESH).start()
-        zrecv[:, pl.ds(z * 2, 2)] = zsend[:, cls]
-        arrived(zrecv.at[:, pl.ds(0, 2 * NZ - 2)], zrecv_sem)
-
-        for j in range(2):
+        odd = lax.rem(z, 2)
+        for q in Z_ORDER:
+            @pl.when(z != q)
+            def _():
+                pltpu.make_async_remote_copy(
+                    src_ref=zsend.at[:, q % 2], dst_ref=zrecv.at[:, pl.ds(pl.multiple_of(z * 4, 4), 4)],
+                    send_sem=zsend_sem, recv_sem=zrecv_sem, device_id=(q * NY + y, s), device_id_type=MESH).start()
+
+        zrecv[:, pl.ds(pl.multiple_of(z * 4, 4), 4)] = zsend[:, odd]
+        arrived(zrecv.at[:, pl.ds(0, 4 * NZ - 4)], zrecv_sem)
+
+        for j in range(4):
             mat = full(first_rows([zrecv[i, 8 * j:8 * j + 8] for i in range(COORDS)]))
             for r in range(3):
                 for c in range(3):
@@ -240,7 +281,7 @@
                         zmat[(r * 3 + c) * 2 + p, 8 * j:8 * j + 8] = mat[r][c][p]
 
         def slab(j):
-            return [[tuple(zmat[(r * 3 + c) * 2 + p, 2 * j:2 * j + 2] for p in range(2)) for c in range(3)]
+            return [[tuple(zmat[(r * 3 + c) * 2 + p, 4 * j:4 * j + 4] for p in range(2)) for c in range(3)]
                     for r in range(3)]
 
         acc = slab(0)[:ROWS]
@@ -263,8 +304,8 @@
         @pl.when(holder)
         def _():
             for to in range(2):
-                phold[to, 0:1] = re[to:to + 1]
-                phold[to, 1:2] = im[to:to + 1]
+                for p, value in enumerate((re, im)):
+                    phold[to, p:p + 1] = jnp.where(lax.rem(z, NCLASS) < 2, value[to:to + 1], value[2 + to:3 + to])
             other = 1 - 2 * half
             for to, where in ((0, (tm, s - 1)), (0, (tm + other, s - 1)), (1, (tm + other, s))):
                 pltpu.make_async_remote_copy(
@@ -273,10 +314,10 @@
             prow[...] = phold[1]
 
         arrived(arecv.at[pl.ds(0, NY - 1)], arecv_sem)
-        mine = cls * NX + x
+        mine = odd * NX + x
         brecv[mine] = jnp.sum(arecv[...], axis=0)
         pl.semaphore_wait(near_sem.at[2], 1)
-        for dz in (2, -1, 1, 0):
+        for dz in (1, 0):
             for dx in (2, 1, 3, 0):
                 for to in (0, 1):
                     if dz != 0 or dx != 0 or to == 0:
@@ -288,12 +329,18 @@
         def _():
             arrived(prow, precv_sem)
 
-        arrived(brecv.at[pl.ds(0, NCLASS * NX - 1)], brecv_sem)
+        arrived(brecv.at[pl.ds(0, 2 * NX - 1)], brecv_sem)
         sent(ysend.at[pl.ds(0, NY - 1)], ysend_sem)
-        sent(zrecv.at[:, pl.ds(0, 2 * NZ - 2)], zsend_sem)
+        for _, _, by, _, cores in RELAYED:
+            @pl.when(y == by)
+            def _():
+                for _ in cores:
+                    sent(yvia.at[0, 0], vsend_sem)
+
+        sent(zrecv.at[:, pl.ds(0, 4 * NZ - 4)], zsend_sem)
         sent(arecv.at[pl.ds(0, NY - 1)], asend_sem)
         sent(brecv, bsend_sem)
-        sent(brecv.at[pl.ds(0, NCLASS * NX - 1)], bsend_sem)
+        sent(brecv.at[pl.ds(0, 2 * NX - 1)], bsend_sem)
 
         @pl.when(holder)
         def _():
@@ -332,17 +379,18 @@
         scratch_shapes=[
             pltpu.VMEM((4, 4, 18, 8, LANES), f32),
             pltpu.VMEM((NY, COORDS, NCLASS, LANES), f32),
+            pltpu.VMEM((2, 2, COORDS, NCLASS, LANES), f32),
             pltpu.VMEM((NY, COORDS, 2 * NCLASS, LANES), f32),
             pltpu.VMEM((NY, 18, 2 * NCLASS, LANES), f32),
-            pltpu.VMEM((COORDS, NCLASS, 2, LANES), f32),
-            pltpu.VMEM((COORDS, 2 * NZ, LANES), f32),
-            pltpu.VMEM((18, 2 * NZ, LANES), f32),
+            pltpu.VMEM((COORDS, 2, 4, LANES), f32),
+            pltpu.VMEM((COORDS, 4 * NZ, LANES), f32),
+            pltpu.VMEM((18, 4 * NZ, LANES), f32),
             pltpu.VMEM((2, 2, LANES), f32),
             pltpu.VMEM((2, LANES), f32),
             pltpu.VMEM((NY, 1, LANES), f32),
-            pltpu.VMEM((NCLASS * NX, 1, LANES), f32),
+            pltpu.VMEM((2 * NX, 1, LANES), f32),
             pltpu.SemaphoreType.REGULAR((3,)),
-            dma((4,)), dma, dma((NY, 2)), dma, dma, dma, dma, dma, dma, dma, dma,
+            dma((4,)), dma((2, 2)), dma, dma, dma((NY, 2)), dma, dma, dma, dma, dma, dma, dma, dma,
         ],
         compiler_params=pltpu.CompilerParams(collective_id=0, has_side_effects=True),
     )(view)

time: 33.2 us -> 32.7 us (0.985)
  Pallas kernels: 32.4 us -> 31.9 us
    pallas_call x1, Pallas kernels: 31.8 us -> 31.3 us  [on_device(): pl.pallas_call(kernel, out_shape=(pltpu.VMEM((2, sites // 64), f32), pltp...]
where the time goes in v5:
time: 32.7 us; the launch traced here: 32.5 us
  Pallas kernels  31.9 us (98%)
  between operations  0.64 us (2%)
    pallas_call x1, Pallas kernels, on_device(): pl.pallas_call(kernel, out_shape=(pltpu.VMEM((2, sites // 64), f32), pltp...  31.3 us

profile of v5, /device:TPU:1, one launch (start us, length us, event | category | flops | bytes accessed | tf_op | source)
XLA Modules:
  0.0 32.5 jit_solution(17984091466966010716)
XLA Ops:
  0.6 31.3 %shard_map.30 = (f32[2,64]{1,0:T(2,128)S(1)}, f32[3]{0:T(128)S(1)}) custom-call(f32[18,8,4,4,128]{4,3,2,1,0:T(4,128)} %bitcast.5), custom_call_target="tpu_custom_call" | custom-call | tf_op jit(solution)/shard_map/pallas_call | solution.py:374
  31.9 0.6 %shard_map.31 = (f32[2,64]{1,0:T(2,128)}, f32[3]{0:T(128)}) custom-call(f32[2,64]{1,0:T(2,128)S(1)} %get-tuple-element.4.ploop_in, f32[3]{0:T(128)S(1)} %get-tuple-element.5.stats_in), custom_call_target="tpu_custom_call" | custom-call | tf_op jit(solution)/shard_map/pallas_call | solution.py:398

commit v6 on v5

--- a/solution.py
+++ b/solution.py
@@ -16,6 +16,7 @@
 COORDS = 8
 FAR_FIRST = (4, 3, 5, 2, 6, 1, 7)
 Z_ORDER = (0, 7, 6, 1, 5, 2, 4, 3)
+SUM_ORDER = (0, 1, 7, 2, 6, 3, 5, 4)
 RELAYED = ((0, 4, 2, 0, (1,)), (0, 4, 6, 1, (0,)), (0, 5, 6, 0, (0, 1)), (7, 4, 5, 0, (0, 1)))
 PAIRS = (2, 1, 3, 0)
 
@@ -111,9 +112,9 @@
     return [two[0], two[1], third_row(two[0], two[1])]
 
 
-def kernel(links, ploop_out, stats_out, lbuf, ysend, yvia, yrecv, ymat, zsend, zrecv, zmat, phold, prow, arecv, brecv,
+def kernel(links, ploop_out, stats_out, lbuf, ysend, yvia, yrecv, ymat, zsend, zrecv, zmat, phold, prow, srow, rows,
            near_sem, load_sem, via_sem, vsend_sem, ysend_sem, yrecv_sem, zsend_sem, zrecv_sem, psend_sem, precv_sem,
-           asend_sem, arecv_sem, bsend_sem, brecv_sem):
+           asend_sem, arecv_sem):
     tm = lax.axis_index("tm")
     s = lax.axis_index("space")
     z = lax.div(tm, NY)
@@ -152,7 +153,7 @@
     def _():
         tell(barrier, [at(0, 0, 0, 1)])
 
-    pairs = [lax.rem(lax.div(y, 2) + step, 4) for step in PAIRS]
+    pairs = PAIRS
     for k, m in enumerate(pairs):
         for t in range(4):
             pltpu.make_async_copy(links.at[:, :, m, t], lbuf.at[k, t], load_sem.at[k]).start()
@@ -186,7 +187,7 @@
                 tell(near_sem.at[0], near)
 
         for start, end, by, slot, cores in RELAYED:
-            if k == (2 if start == 7 else 0):
+            if k == 0:
                 @pl.when((y == start) & ((core == cores[0]) | (core == cores[-1])))
                 def _():
                     pltpu.make_async_remote_copy(
@@ -225,7 +226,7 @@
     @pl.when(core == 0)
     def _():
         arrived(prow, precv_sem)
-        arrived(brecv, brecv_sem)
+        arrived(rows, arecv_sem)
         sent(ysend, ysend_sem)
 
     @pl.when(core == 1)
@@ -261,7 +262,7 @@
                     zsend[i, k % 2, at_row:at_row + 1] = v[row:row + 1]
 
         pl.semaphore_wait(near_sem.at[1], len(farther))
-        tell(near_sem.at[2], [at(0, 0, 2, 1)])
+        tell(near_sem.at[2], [at(0, 0, dx, 1) for dx in (2, 1, 3)] + [at(-1, 0, dx, 1) for dx in range(NX)])
         odd = lax.rem(z, 2)
         for q in Z_ORDER:
             @pl.when(z != q)
@@ -295,12 +296,27 @@
             return jnp.sum(jnp.sum(value, axis=1, keepdims=True), axis=0, keepdims=True)
 
         sums = jnp.where(lane == 0, total(re), jnp.where(lane == 1, total(im), total(re * re + im * im)))
-        arecv[y] = sums
-        for d in FAR_FIRST:
-            pltpu.make_async_remote_copy(
-                src_ref=arecv.at[y], dst_ref=arecv.at[y], send_sem=asend_sem,
-                recv_sem=arecv_sem, device_id=at(0, d, 0, 1), device_id_type=MESH).start()
-
+        mine = (odd * NX + x) * NY + y
+        srow[...] = sums
+        pl.semaphore_wait(near_sem.at[2], 2 * NX - 1)
+        last = z == NZ - 1
+        for step in (0, 1):
+            dz = jnp.where(last, 1 - step, step)
+            for q in SUM_ORDER:
+                for dx in (2, 1, 3, 0):
+                    for to in (1, 0):
+                        def send():
+                            pltpu.make_async_remote_copy(
+                                src_ref=srow, dst_ref=rows.at[pl.ds(mine, 1)], send_sem=asend_sem, recv_sem=arecv_sem,
+                                device_id=(lax.rem(z + dz, NZ) * NY + q, lax.rem(x + dx, NX) * 2 + to),
+                                device_id_type=MESH).start()
+
+                        if dx == 0 and to == 1:
+                            pl.when((dz != 0) | (y != q))(send)
+                        else:
+                            send()
+
+        rows[pl.ds(mine, 1)] = sums
         @pl.when(holder)
         def _():
             for to in range(2):
@@ -313,23 +329,11 @@
                     device_id=where, device_id_type=MESH).start()
             prow[...] = phold[1]
 
-        arrived(arecv.at[pl.ds(0, NY - 1)], arecv_sem)
-        mine = odd * NX + x
-        brecv[mine] = jnp.sum(arecv[...], axis=0)
-        pl.semaphore_wait(near_sem.at[2], 1)
-        for dz in (1, 0):
-            for dx in (2, 1, 3, 0):
-                for to in (0, 1):
-                    if dz != 0 or dx != 0 or to == 0:
-                        pltpu.make_async_remote_copy(
-                            src_ref=brecv.at[mine], dst_ref=brecv.at[mine], send_sem=bsend_sem,
-                            recv_sem=brecv_sem, device_id=at(dz, 0, dx, to), device_id_type=MESH).start()
-
         @pl.when(jnp.logical_not(holder))
         def _():
             arrived(prow, precv_sem)
 
-        arrived(brecv.at[pl.ds(0, 2 * NX - 1)], brecv_sem)
+        arrived(rows.at[pl.ds(0, 2 * NX * NY - 1)], arecv_sem)
         sent(ysend.at[pl.ds(0, NY - 1)], ysend_sem)
         for _, _, by, _, cores in RELAYED:
             @pl.when(y == by)
@@ -338,9 +342,8 @@
                     sent(yvia.at[0, 0], vsend_sem)
 
         sent(zrecv.at[:, pl.ds(0, 4 * NZ - 4)], zsend_sem)
-        sent(arecv.at[pl.ds(0, NY - 1)], asend_sem)
-        sent(brecv, bsend_sem)
-        sent(brecv.at[pl.ds(0, 2 * NX - 1)], bsend_sem)
+        sent(rows, asend_sem)
+        sent(rows.at[pl.ds(0, 2 * NX * NY - 1)], asend_sem)
 
         @pl.when(holder)
         def _():
@@ -348,7 +351,7 @@
                 sent(prow, psend_sem)
 
     ploop_out[...] = jnp.where(half == 0, prow[:, :64], prow[:, 64:])
-    grand = jnp.sum(brecv[...], axis=0) / (NY * NCLASS * NSPACE * LANES)
+    grand = jnp.sum(rows[...], axis=0, keepdims=True) / (NY * NCLASS * NSPACE * LANES)
     means = jnp.where(lane < 2, grand * grand, 0.0)
     stats = grand - jnp.where(lane == 2, jnp.sum(means, axis=1, keepdims=True), 0.0)
     stats_out[...] = stats[0, :3]
@@ -387,10 +390,10 @@
             pltpu.VMEM((18, 4 * NZ, LANES), f32),
             pltpu.VMEM((2, 2, LANES), f32),
             pltpu.VMEM((2, LANES), f32),
-            pltpu.VMEM((NY, 1, LANES), f32),
-            pltpu.VMEM((2 * NX, 1, LANES), f32),
+            pltpu.VMEM((1, LANES), f32),
+            pltpu.VMEM((2 * NX * NY, LANES), f32),
             pltpu.SemaphoreType.REGULAR((3,)),
-            dma((4,)), dma((2, 2)), dma, dma, dma((NY, 2)), dma, dma, dma, dma, dma, dma, dma, dma,
+            dma((4,)), dma((2, 2)), dma, dma, dma((NY, 2)), dma, dma, dma, dma, dma, dma,
         ],
         compiler_params=pltpu.CompilerParams(collective_id=0, has_side_effects=True),
     )(view)

time: 32.7 us -> 31.5 us (0.963)
  Pallas kernels: 31.9 us -> 30.6 us
    pallas_call x1, Pallas kernels: 31.3 us -> 30 us  [on_device(): pl.pallas_call(kernel, out_shape=(pltpu.VMEM((2, sites // 64), f32), pltp...]
where the time goes in v6:
time: 31.5 us; the launch traced here: 31.3 us
  Pallas kernels  30.6 us (97%)
  between operations  0.64 us (2%)
    pallas_call x1, Pallas kernels, on_device(): pl.pallas_call(kernel, out_shape=(pltpu.VMEM((2, sites // 64), f32), pltp...  30 us

profile of v6, /device:TPU:1, one launch (start us, length us, event | category | flops | bytes accessed | tf_op | source)
XLA Modules:
  0.0 31.3 jit_solution(12142799437436125293)
XLA Ops:
  0.6 30.0 %shard_map.30 = (f32[2,64]{1,0:T(2,128)S(1)}, f32[3]{0:T(128)S(1)}) custom-call(f32[18,8,4,4,128]{4,3,2,1,0:T(4,128)} %bitcast.5), custom_call_target="tpu_custom_call" | custom-call | tf_op jit(solution)/shard_map/pallas_call | solution.py:377
  30.7 0.6 %shard_map.31 = (f32[2,64]{1,0:T(2,128)}, f32[3]{0:T(128)}) custom-call(f32[2,64]{1,0:T(2,128)S(1)} %get-tuple-element.4.ploop_in, f32[3]{0:T(128)S(1)} %get-tuple-element.5.stats_in), custom_call_target="tpu_custom_call" | custom-call | tf_op jit(solution)/shard_map/pallas_call | solution.py:401

commit v7 on v6

--- a/solution.py
+++ b/solution.py
@@ -16,6 +16,8 @@
 COORDS = 8
 FAR_FIRST = (4, 3, 5, 2, 6, 1, 7)
 Z_ORDER = (0, 7, 6, 1, 5, 2, 4, 3)
+EARLY = 3
+PASS_ON = ((2, (3, 4, 5, 6, 7)),)
 SUM_ORDER = (0, 1, 7, 2, 6, 3, 5, 4)
 RELAYED = ((0, 4, 2, 0, (1,)), (0, 4, 6, 1, (0,)), (0, 5, 6, 0, (0, 1)), (7, 4, 5, 0, (0, 1)))
 PAIRS = (2, 1, 3, 0)
@@ -112,9 +114,9 @@
     return [two[0], two[1], third_row(two[0], two[1])]
 
 
-def kernel(links, ploop_out, stats_out, lbuf, ysend, yvia, yrecv, ymat, zsend, zrecv, zmat, phold, prow, srow, rows,
+def kernel(links, ploop_out, stats_out, lbuf, ysend, yvia, yrecv, ymat, zsend, zrecv, zmat, phold, prow, srow, rows, final,
            near_sem, load_sem, via_sem, vsend_sem, ysend_sem, yrecv_sem, zsend_sem, zrecv_sem, psend_sem, precv_sem,
-           asend_sem, arecv_sem):
+           asend_sem, arecv_sem, gsend_sem, grecv_sem):
     tm = lax.axis_index("tm")
     s = lax.axis_index("space")
     z = lax.div(tm, NY)
@@ -226,7 +228,8 @@
     @pl.when(core == 0)
     def _():
         arrived(prow, precv_sem)
-        arrived(rows, arecv_sem)
+        pl.when(z < EARLY)(lambda: arrived(rows, arecv_sem))
+        pl.when(z >= EARLY)(lambda: arrived(final, grecv_sem))
         sent(ysend, ysend_sem)
 
     @pl.when(core == 1)
@@ -302,19 +305,22 @@
         last = z == NZ - 1
         for step in (0, 1):
             dz = jnp.where(last, 1 - step, step)
-            for q in SUM_ORDER:
-                for dx in (2, 1, 3, 0):
-                    for to in (1, 0):
-                        def send():
-                            pltpu.make_async_remote_copy(
-                                src_ref=srow, dst_ref=rows.at[pl.ds(mine, 1)], send_sem=asend_sem, recv_sem=arecv_sem,
-                                device_id=(lax.rem(z + dz, NZ) * NY + q, lax.rem(x + dx, NX) * 2 + to),
-                                device_id_type=MESH).start()
-
-                        if dx == 0 and to == 1:
-                            pl.when((dz != 0) | (y != q))(send)
-                        else:
-                            send()
+            end = lax.rem(z + dz, NZ)
+
+            @pl.when(end < EARLY)
+            def _():
+                for q in SUM_ORDER:
+                    for dx in (2, 1, 3, 0):
+                        for to in (1, 0):
+                            def send():
+                                pltpu.make_async_remote_copy(
+                                    src_ref=srow, dst_ref=rows.at[pl.ds(mine, 1)], send_sem=asend_sem, recv_sem=arecv_sem,
+                                    device_id=(end * NY + q, lax.rem(x + dx, NX) * 2 + to), device_id_type=MESH).start()
+
+                            if dx == 0 and to == 1:
+                                pl.when((dz != 0) | (y != q))(send)
+                            else:
+                                send()
 
         rows[pl.ds(mine, 1)] = sums
         @pl.when(holder)
@@ -333,7 +339,8 @@
         def _():
             arrived(prow, precv_sem)
 
-        arrived(rows.at[pl.ds(0, 2 * NX * NY - 1)], arecv_sem)
+        pl.when(z < EARLY)(lambda: arrived(rows.at[pl.ds(0, 2 * NX * NY - 1)], arecv_sem))
+        pl.when(z >= EARLY)(lambda: arrived(final, grecv_sem))
         sent(ysend.at[pl.ds(0, NY - 1)], ysend_sem)
         for _, _, by, _, cores in RELAYED:
             @pl.when(y == by)
@@ -342,8 +349,8 @@
                     sent(yvia.at[0, 0], vsend_sem)
 
         sent(zrecv.at[:, pl.ds(0, 4 * NZ - 4)], zsend_sem)
-        sent(rows, asend_sem)
-        sent(rows.at[pl.ds(0, 2 * NX * NY - 1)], asend_sem)
+        pl.when((z < EARLY - 1) | last)(lambda: sent(rows, asend_sem))
+        pl.when(z < EARLY)(lambda: sent(rows.at[pl.ds(0, 2 * NX * NY - 1)], asend_sem))
 
         @pl.when(holder)
         def _():
@@ -351,10 +358,23 @@
                 sent(prow, psend_sem)
 
     ploop_out[...] = jnp.where(half == 0, prow[:, :64], prow[:, 64:])
-    grand = jnp.sum(rows[...], axis=0, keepdims=True) / (NY * NCLASS * NSPACE * LANES)
-    means = jnp.where(lane < 2, grand * grand, 0.0)
-    stats = grand - jnp.where(lane == 2, jnp.sum(means, axis=1, keepdims=True), 0.0)
-    stats_out[...] = stats[0, :3]
+    @pl.when(z < EARLY)
+    def _():
+        grand = jnp.sum(rows[...], axis=0, keepdims=True) / (NY * NCLASS * NSPACE * LANES)
+        means = jnp.where(lane < 2, grand * grand, 0.0)
+        final[...] = grand - jnp.where(lane == 2, jnp.sum(means, axis=1, keepdims=True), 0.0)
+
+    for start, ends in PASS_ON:
+        @pl.when((core == 1) & (z == start))
+        def _():
+            for end in ends:
+                for to in (1, 0):
+                    pltpu.make_async_remote_copy(
+                        src_ref=final, dst_ref=final, send_sem=gsend_sem, recv_sem=grecv_sem,
+                        device_id=(end * NY + y, x * 2 + to), device_id_type=MESH).start()
+            sent(rows.at[pl.ds(0, 2 * len(ends))], gsend_sem)
+
+    stats_out[...] = final[0, :3]
 
 
 def finish(ploop_in, stats_in, ploop_out, stats_out, sems):
@@ -392,8 +412,9 @@
             pltpu.VMEM((2, LANES), f32),
             pltpu.VMEM((1, LANES), f32),
             pltpu.VMEM((2 * NX * NY, LANES), f32),
+            pltpu.VMEM((1, LANES), f32),
             pltpu.SemaphoreType.REGULAR((3,)),
-            dma((4,)), dma((2, 2)), dma, dma, dma((NY, 2)), dma, dma, dma, dma, dma, dma,
+            dma((4,)), dma((2, 2)), dma, dma, dma((NY, 2)), dma, dma, dma, dma, dma, dma, dma, dma,
         ],
         compiler_params=pltpu.CompilerParams(collective_id=0, has_side_effects=True),
     )(view)

time: 31.5 us -> 31.2 us (level)
  no operation moved by 1% of the time
where the time goes in v7:
time: 31.2 us; the launch traced here: 31 us
  Pallas kernels  30.4 us (97%)
  between operations  0.64 us (2%)
    pallas_call x1, Pallas kernels, on_device(): pl.pallas_call(kernel, out_shape=(pltpu.VMEM((2, sites // 64), f32), pltp...  29.8 us

profile of v7, /device:TPU:1, one launch (start us, length us, event | category | flops | bytes accessed | tf_op | source)
XLA Modules:
  0.0 31.0 jit_solution(15063636197593236723)
XLA Ops:
  0.6 29.8 %shard_map.30 = (f32[2,64]{1,0:T(2,128)S(1)}, f32[3]{0:T(128)S(1)}) custom-call(f32[18,8,4,4,128]{4,3,2,1,0:T(4,128)} %bitcast.5), custom_call_target="tpu_custom_call" | custom-call | tf_op jit(solution)/shard_map/pallas_call | solution.py:397
  30.4 0.6 %shard_map.31 = (f32[2,64]{1,0:T(2,128)}, f32[3]{0:T(128)}) custom-call(f32[2,64]{1,0:T(2,128)S(1)} %get-tuple-element.4.ploop_in, f32[3]{0:T(128)S(1)} %get-tuple-element.5.stats_in), custom_call_target="tpu_custom_call" | custom-call | tf_op jit(solution)/shard_map/pallas_call | solution.py:422

commit v8 on v7

--- a/solution.py
+++ b/solution.py
@@ -114,9 +114,9 @@
     return [two[0], two[1], third_row(two[0], two[1])]
 
 
-def kernel(links, ploop_out, stats_out, lbuf, ysend, yvia, yrecv, ymat, zsend, zrecv, zmat, phold, prow, srow, rows, final,
-           near_sem, load_sem, via_sem, vsend_sem, ysend_sem, yrecv_sem, zsend_sem, zrecv_sem, psend_sem, precv_sem,
-           asend_sem, arecv_sem, gsend_sem, grecv_sem):
+def kernel(links, ploop_out, stats_out, lbuf, ysend, yvia, yrecv, ymat, zsend, zrecv, phold, prow, srow, rows, final,
+           near_sem, load_sem, via_sem, ysend_sem, yrecv_sem, zsend_sem, zrecv_sem, precv_sem,
+           asend_sem, arecv_sem, grecv_sem):
     tm = lax.axis_index("tm")
     s = lax.axis_index("space")
     z = lax.div(tm, NY)
@@ -177,7 +177,7 @@
     def ycopy(q):
         pltpu.make_async_remote_copy(
             src_ref=ysend.at[q], dst_ref=yrecv.at[y, :, pl.ds(pl.multiple_of(core * NCLASS, NCLASS), NCLASS)],
-            send_sem=ysend_sem, recv_sem=yrecv_sem.at[y, core], device_id=(z * NY + q, x * 2 + 1), device_id_type=MESH).start()
+            send_sem=ysend_sem, recv_sem=yrecv_sem.at[y], device_id=(z * NY + q, x * 2 + 1), device_id_type=MESH).start()
 
     for k in range(4):
         local(k)
@@ -194,7 +194,7 @@
                 def _():
                     pltpu.make_async_remote_copy(
                         src_ref=ysend.at[end], dst_ref=yvia.at[slot, core], send_sem=ysend_sem,
-                        recv_sem=via_sem.at[slot, core], device_id=(z * NY + by, x * 2 + 1),
+                        recv_sem=via_sem.at[slot], device_id=(z * NY + by, x * 2 + 1),
                         device_id_type=MESH).start()
 
         for h in range(2):
@@ -241,18 +241,16 @@
         for start, end, by, slot, cores in RELAYED:
             @pl.when(y == by)
             def _():
+                arrived(yvia.at[slot] if len(cores) == 2 else yvia.at[slot, cores[0]], via_sem.at[slot])
                 for to in cores:
-                    arrived(yvia.at[slot, to], via_sem.at[slot, to])
                     pltpu.make_async_remote_copy(
                         src_ref=yvia.at[slot, to], dst_ref=yrecv.at[start, :, pl.ds(NCLASS * to, NCLASS)],
-                        send_sem=vsend_sem, recv_sem=yrecv_sem.at[start, to], device_id=(z * NY + end, s),
+                        send_sem=ysend_sem, recv_sem=yrecv_sem.at[start], device_id=(z * NY + end, s),
                         device_id_type=MESH).start()
 
         for d in FAR_FIRST + (0,):
             j = lax.rem(y + d, NY)
-            arrived(yrecv.at[j, :, pl.ds(0, NCLASS)], yrecv_sem.at[j, 0])
-            if d != 0:
-                arrived(yrecv.at[j, :, pl.ds(NCLASS, NCLASS)], yrecv_sem.at[j, 1])
+            arrived(yrecv.at[j] if d != 0 else yrecv.at[j, :, pl.ds(0, NCLASS)], yrecv_sem.at[j])
             store(ymat, j, full(first_rows([yrecv[j, i] for i in range(COORDS)])))
         acc = load(ymat, 0)[:ROWS]
         for j in range(1, NY):
@@ -267,30 +265,21 @@
         pl.semaphore_wait(near_sem.at[1], len(farther))
         tell(near_sem.at[2], [at(0, 0, dx, 1) for dx in (2, 1, 3)] + [at(-1, 0, dx, 1) for dx in range(NX)])
         odd = lax.rem(z, 2)
+        place = pl.multiple_of((odd * 4 + lax.div(z, 4) + lax.rem(lax.div(z, 2), 2) * 2) * 4, 4)
         for q in Z_ORDER:
             @pl.when(z != q)
             def _():
                 pltpu.make_async_remote_copy(
-                    src_ref=zsend.at[:, q % 2], dst_ref=zrecv.at[:, pl.ds(pl.multiple_of(z * 4, 4), 4)],
+                    src_ref=zsend.at[:, q % 2], dst_ref=zrecv.at[:, pl.ds(place, 4)],
                     send_sem=zsend_sem, recv_sem=zrecv_sem, device_id=(q * NY + y, s), device_id_type=MESH).start()
 
-        zrecv[:, pl.ds(pl.multiple_of(z * 4, 4), 4)] = zsend[:, odd]
+        zrecv[:, pl.ds(place, 4)] = zsend[:, odd]
         arrived(zrecv.at[:, pl.ds(0, 4 * NZ - 4)], zrecv_sem)
 
-        for j in range(4):
-            mat = full(first_rows([zrecv[i, 8 * j:8 * j + 8] for i in range(COORDS)]))
-            for r in range(3):
-                for c in range(3):
-                    for p in range(2):
-                        zmat[(r * 3 + c) * 2 + p, 8 * j:8 * j + 8] = mat[r][c][p]
-
-        def slab(j):
-            return [[tuple(zmat[(r * 3 + c) * 2 + p, 4 * j:4 * j + 4] for p in range(2)) for c in range(3)]
-                    for r in range(3)]
-
-        acc = slab(0)[:ROWS]
-        for j in range(1, NZ):
-            acc = times(acc, slab(j))
+        parts = [first_rows([zrecv[i, 8 * j:8 * j + 8] for i in range(COORDS)]) for j in range(4)]
+        quads = times(times(parts[0], full(parts[2])), full(times(parts[1], full(parts[3]))))
+        left, right = ([[tuple(v[at_row:at_row + 4] for v in pair) for pair in row] for row in quads] for at_row in (0, 4))
+        acc = times(left, full(right))
         whole = full(acc)
         re = (whole[0][0][0] + whole[1][1][0] + whole[2][2][0]) / 3.0
         im = (whole[0][0][1] + whole[1][1][1] + whole[2][2][1]) / 3.0
@@ -309,16 +298,16 @@
 
             @pl.when(end < EARLY)
             def _():
-                for q in SUM_ORDER:
-                    for dx in (2, 1, 3, 0):
-                        for to in (1, 0):
+                for to in (1, 0):
+                    for q in SUM_ORDER:
+                        for to_x in (0, 1, 3, 2):
                             def send():
                                 pltpu.make_async_remote_copy(
                                     src_ref=srow, dst_ref=rows.at[pl.ds(mine, 1)], send_sem=asend_sem, recv_sem=arecv_sem,
-                                    device_id=(end * NY + q, lax.rem(x + dx, NX) * 2 + to), device_id_type=MESH).start()
-
-                            if dx == 0 and to == 1:
-                                pl.when((dz != 0) | (y != q))(send)
+                                    device_id=(end * NY + q, to_x * 2 + to), device_id_type=MESH).start()
+
+                            if to == 1:
+                                pl.when((dz != 0) | (y != q) | (x != to_x))(send)
                             else:
                                 send()
 
@@ -331,7 +320,7 @@
             other = 1 - 2 * half
             for to, where in ((0, (tm, s - 1)), (0, (tm + other, s - 1)), (1, (tm + other, s))):
                 pltpu.make_async_remote_copy(
-                    src_ref=phold.at[to], dst_ref=prow, send_sem=psend_sem, recv_sem=precv_sem,
+                    src_ref=phold.at[to], dst_ref=prow, send_sem=asend_sem, recv_sem=precv_sem,
                     device_id=where, device_id_type=MESH).start()
             prow[...] = phold[1]
 
@@ -346,7 +335,7 @@
             @pl.when(y == by)
             def _():
                 for _ in cores:
-                    sent(yvia.at[0, 0], vsend_sem)
+                    sent(yvia.at[0, 0], ysend_sem)
 
         sent(zrecv.at[:, pl.ds(0, 4 * NZ - 4)], zsend_sem)
         pl.when((z < EARLY - 1) | last)(lambda: sent(rows, asend_sem))
@@ -355,7 +344,7 @@
         @pl.when(holder)
         def _():
             for _ in range(3):
-                sent(prow, psend_sem)
+                sent(prow, asend_sem)
 
     ploop_out[...] = jnp.where(half == 0, prow[:, :64], prow[:, 64:])
     @pl.when(z < EARLY)
@@ -370,9 +359,9 @@
             for end in ends:
                 for to in (1, 0):
                     pltpu.make_async_remote_copy(
-                        src_ref=final, dst_ref=final, send_sem=gsend_sem, recv_sem=grecv_sem,
+                        src_ref=final, dst_ref=final, send_sem=asend_sem, recv_sem=grecv_sem,
                         device_id=(end * NY + y, x * 2 + to), device_id_type=MESH).start()
-            sent(rows.at[pl.ds(0, 2 * len(ends))], gsend_sem)
+            sent(rows.at[pl.ds(0, 2 * len(ends))], asend_sem)
 
     stats_out[...] = final[0, :3]
 
@@ -407,14 +396,13 @@
             pltpu.VMEM((NY, 18, 2 * NCLASS, LANES), f32),
             pltpu.VMEM((COORDS, 2, 4, LANES), f32),
             pltpu.VMEM((COORDS, 4 * NZ, LANES), f32),
-            pltpu.VMEM((18, 4 * NZ, LANES), f32),
             pltpu.VMEM((2, 2, LANES), f32),
             pltpu.VMEM((2, LANES), f32),
             pltpu.VMEM((1, LANES), f32),
             pltpu.VMEM((2 * NX * NY, LANES), f32),
             pltpu.VMEM((1, LANES), f32),
             pltpu.SemaphoreType.REGULAR((3,)),
-            dma((4,)), dma((2, 2)), dma, dma, dma((NY, 2)), dma, dma, dma, dma, dma, dma, dma, dma,
+            dma((4,)), dma((2,)), dma, dma((NY,)), dma, dma, dma, dma, dma, dma,
         ],
         compiler_params=pltpu.CompilerParams(collective_id=0, has_side_effects=True),
     )(view)

time: 31.2 us -> 31 us (level)
  no operation moved by 1% of the time
where the time goes in v8:
time: 31 us; the launch traced here: 30.8 us
  Pallas kernels  30.2 us (97%)
  between operations  0.64 us (2%)
    pallas_call x1, Pallas kernels, on_device(): pl.pallas_call(kernel, out_shape=(pltpu.VMEM((2, sites // 64), f32), pltp...  29.6 us

profile of v8, /device:TPU:1, one launch (start us, length us, event | category | flops | bytes accessed | tf_op | source)
XLA Modules:
  0.0 30.8 jit_solution(16087035334871981492)
XLA Ops:
  0.6 29.6 %shard_map.30 = (f32[2,64]{1,0:T(2,128)S(1)}, f32[3]{0:T(128)S(1)}) custom-call(f32[18,8,4,4,128]{4,3,2,1,0:T(4,128)} %bitcast.5), custom_call_target="tpu_custom_call" | custom-call | tf_op jit(solution)/shard_map/pallas_call | solution.py:386
  30.2 0.6 %shard_map.31 = (f32[2,64]{1,0:T(2,128)}, f32[3]{0:T(128)}) custom-call(f32[2,64]{1,0:T(2,128)S(1)} %get-tuple-element.4.ploop_in, f32[3]{0:T(128)S(1)} %get-tuple-element.5.stats_in), custom_call_target="tpu_custom_call" | custom-call | tf_op jit(solution)/shard_map/pallas_call | solution.py:410

commit v9 on v8

--- a/solution.py
+++ b/solution.py
@@ -21,6 +21,7 @@
 SUM_ORDER = (0, 1, 7, 2, 6, 3, 5, 4)
 RELAYED = ((0, 4, 2, 0, (1,)), (0, 4, 6, 1, (0,)), (0, 5, 6, 0, (0, 1)), (7, 4, 5, 0, (0, 1)))
 PAIRS = (2, 1, 3, 0)
+PAIRS_0 = (2, 3, 1, 0)
 
 
 def third_row(a, b):
@@ -155,7 +156,7 @@
     def _():
         tell(barrier, [at(0, 0, 0, 1)])
 
-    pairs = PAIRS
+    pairs = [jnp.where(core == 1, m, n) for m, n in zip(PAIRS, PAIRS_0)]
     for k, m in enumerate(pairs):
         for t in range(4):
             pltpu.make_async_copy(links.at[:, :, m, t], lbuf.at[k, t], load_sem.at[k]).start()

time: 31 us -> 31 us (level)
  no operation moved by 1% of the time
where the time goes in v9:
time: 31 us; the launch traced here: 30.9 us
  Pallas kernels  30.2 us (97%)
  between operations  0.64 us (2%)
    pallas_call x1, Pallas kernels, on_device(): pl.pallas_call(kernel, out_shape=(pltpu.VMEM((2, sites // 64), f32), pltp...  29.6 us

profile of v9, /device:TPU:1, one launch (start us, length us, event | category | flops | bytes accessed | tf_op | source)
XLA Modules:
  0.0 30.9 jit_solution(3831954117951252506)
XLA Ops:
  0.6 29.6 %shard_map.30 = (f32[2,64]{1,0:T(2,128)S(1)}, f32[3]{0:T(128)S(1)}) custom-call(f32[18,8,4,4,128]{4,3,2,1,0:T(4,128)} %bitcast.5), custom_call_target="tpu_custom_call" | custom-call | tf_op jit(solution)/shard_map/pallas_call | solution.py:387
  30.3 0.6 %shard_map.31 = (f32[2,64]{1,0:T(2,128)}, f32[3]{0:T(128)}) custom-call(f32[2,64]{1,0:T(2,128)S(1)} %get-tuple-element.4.ploop_in, f32[3]{0:T(128)S(1)} %get-tuple-element.5.stats_in), custom_call_target="tpu_custom_call" | custom-call | tf_op jit(solution)/shard_map/pallas_call | solution.py:411

commit v10 on v9

--- a/solution.py
+++ b/solution.py
@@ -15,7 +15,7 @@
 ROWS = 2
 COORDS = 8
 FAR_FIRST = (4, 3, 5, 2, 6, 1, 7)
-Z_ORDER = (0, 7, 6, 1, 5, 2, 4, 3)
+Z_ORDER = (0, 7, 1, 2, 6, 5, 4, 3)
 EARLY = 3
 PASS_ON = ((2, (3, 4, 5, 6, 7)),)
 SUM_ORDER = (0, 1, 7, 2, 6, 3, 5, 4)

time: 31 us -> 31 us (level)
  no operation moved by 1% of the time
where the time goes in v10:
time: 31 us; the launch traced here: 30.9 us
  Pallas kernels  30.2 us (97%)
  between operations  0.64 us (2%)
    pallas_call x1, Pallas kernels, on_device(): pl.pallas_call(kernel, out_shape=(pltpu.VMEM((2, sites // 64), f32), pltp...  29.6 us

profile of v10, /device:TPU:1, one launch (start us, length us, event | category | flops | bytes accessed | tf_op | source)
XLA Modules:
  0.0 30.9 jit_solution(2118495036512110235)
XLA Ops:
  0.6 29.6 %shard_map.30 = (f32[2,64]{1,0:T(2,128)S(1)}, f32[3]{0:T(128)S(1)}) custom-call(f32[18,8,4,4,128]{4,3,2,1,0:T(4,128)} %bitcast.5), custom_call_target="tpu_custom_call" | custom-call | tf_op jit(solution)/shard_map/pallas_call | solution.py:387
  30.3 0.6 %shard_map.31 = (f32[2,64]{1,0:T(2,128)}, f32[3]{0:T(128)}) custom-call(f32[2,64]{1,0:T(2,128)S(1)} %get-tuple-element.4.ploop_in, f32[3]{0:T(128)S(1)} %get-tuple-element.5.stats_in), custom_call_target="tpu_custom_call" | custom-call | tf_op jit(solution)/shard_map/pallas_call | solution.py:411
